TPU v7x, 512 devices: a whole 4x8x8 slice. The times are simulated.
512 devices in a mesh: users: 32 (over z, y_hi, core), items: 16 (over y_lo, x).
Axes of the slice: x: 4, y: 8 (y_hi: 2, y_lo: 4; y = y_hi * 4 + y_lo), z: 8, core: 2. Of those that a mesh axis runs over, the one named last changes fastest.
Arguments:
- prefs: int32 [32768, 16384], P('users', 'items'), may hold values from 0 to 4
- item_weight: float32 [16384], P('items'), may hold values from 0.05 to 1.35
- clip_units: int32 [32768], P('users'), may hold values from 100 to 999
- user_emb: float32 [32768, 128], P(('users', 'items')), may hold values from -0.6 to 0.6
- user_acc: float32 [32768, 128], P(('users', 'items')), may hold values from 100 to 3000
- item_emb: float32 [16384, 128], P(('items', 'users')), may hold values from -0.6 to 0.6
- item_acc: float32 [16384, 128], P(('items', 'users')), may hold values from 100 to 3000
- noise: int32 [16384, 128], P(('items', 'users')), may hold values from -1000 to 1000
Outputs:
- new_user_emb: float32 [32768, 128], P(('users', 'items'))
- new_user_acc: float32 [32768, 128], P(('users', 'items'))
- new_item_emb: float32 [16384, 128], P(('items', 'users'))
- new_item_acc: float32 [16384, 128], P(('items', 'users'))
All inputs are finite; a program needn't handle non-finite values.
Results may differ from a plain program's by a relative error of at most 0.0003.
Values sent between devices are 32-bit elements; how exact they have to be, the bound alone decides.
No kernel may reach another device: no remote copies, remote signals or barrier semaphores. Data moves between devices by JAX's collectives and lax.ppermute only.
A program may use at most 64 MiB of HBM per device.

v0:
```python
import jax
import jax.numpy as jnp
from jax import lax
from jax.sharding import PartitionSpec as P

noise_step = 0.05
learn_rate = 0.5


def from_everyone(value, axis):
    peers = lax.axis_size(axis)
    return lax.all_to_all(
        jnp.broadcast_to(value[None], (peers, *value.shape)), axis, 0, 0, tiled=True
    )


def in_order(tiles, dim):
    dims = list(tiles.shape[1:])
    dims[dim] *= tiles.shape[0]
    return jnp.moveaxis(tiles, 0, dim).reshape(dims)


def gather_directly(value, axis, dim):
    tiles = from_everyone(value, axis)
    return in_order(tiles, dim)


def taken_together(value, axis):
    everything = from_everyone(value, axis)
    return jnp.sum(everything, axis=0)


def cut_along(value, dim, peers):
    dims = value.shape
    tiles = value.reshape(*dims[:dim], peers, dims[dim] // peers, *dims[dim + 1 :])
    return jnp.moveaxis(tiles, dim, 0)


def sent_and_summed(value, axis, dim):
    peers = lax.axis_size(axis)
    tiles = lax.all_to_all(cut_along(value, dim, peers), axis, 0, 0, tiled=True)
    return jnp.sum(tiles, axis=0)


def local(prefs, item_weight, clip_units, user_emb, user_acc, item_emb, item_acc, noise):
    precise = lax.Precision.HIGHEST
    user_rows = gather_directly(user_emb, "items", 0)
    num_items = prefs.shape[1]
    width = user_emb.shape[1]
    bound_scale = 0.001 * jnp.sqrt(jnp.float32(num_items * lax.axis_size("items") * width))
    portion = gather_directly(item_emb, "users", 0)
    predicted = lax.dot_general(
        user_rows,
        portion,
        (((1,), (1,)), ((), ())),
        precision=precise,
        preferred_element_type=jnp.float32,
    )
    target = jnp.where(prefs > 0, 1.0, 0.0).astype(jnp.float32)
    confidence = 1.0 + item_weight[None, :] * prefs.astype(jnp.float32)
    weighted = -2.0 * confidence * (target - predicted)
    sq_sum = jnp.sum(weighted * weighted, axis=1)
    gradient = jnp.dot(weighted, portion, precision=precise, preferred_element_type=jnp.float32)
    absorb_stored = weighted
    sq_sum, gradient, stored = (sq_sum, gradient, absorb_stored)
    user_sq = jnp.sum(user_rows * user_rows, axis=1)
    total_sq = taken_together(sq_sum, "items")
    factor = jnp.minimum(
        1.0, clip_units.astype(jnp.float32) * bound_scale / jnp.sqrt(total_sq * user_sq + 1e-06)
    )
    user_grad = sent_and_summed(gradient, "items", 0)
    scaled = user_rows * factor[:, None]
    weighted = stored
    item_sum = sent_and_summed(
        lax.dot_general(
            weighted,
            scaled,
            (((0,), (0,)), ((), ())),
            precision=precise,
            preferred_element_type=jnp.float32,
        ),
        "users",
        0,
    )
    item_grad = item_sum + noise_step * noise.astype(jnp.float32)
    new_user_acc = user_acc + user_grad * user_grad
    new_user_emb = user_emb - learn_rate * user_grad / jnp.sqrt(new_user_acc)
    new_item_acc = item_acc + item_grad * item_grad
    new_item_emb = item_emb - learn_rate * item_grad / jnp.sqrt(new_item_acc)
    return (new_user_emb, new_user_acc, new_item_emb, new_item_acc)


def solution(mesh):
    placed = (
        P("users", "items"),
        P("items"),
        P("users"),
        P(("users", "items"), None),
        P(("users", "items"), None),
        P(("items", "users"), None),
        P(("items", "users"), None),
        P(("items", "users"), None),
    )
    return jax.shard_map(
        local,
        mesh=mesh,
        in_specs=placed,
        out_specs=(
            P(("users", "items"), None),
            P(("users", "items"), None),
            P(("items", "users"), None),
            P(("items", "users"), None),
        ),
        check_vma=False,
    )
```

profile of v0, /device:TPU:8, one launch (start us, length us, event | category | flops | bytes accessed | tf_op | source)
XLA Modules:
  0.0 134.6 jit_solution(14277882512834936913)
XLA Ops:
  0.6 0.8 broadcast_in_dim.13
  1.4 22.4 %all_to_all.26 = f32[16,64,128]{2,1,0:T(8,128)S(1)} all-to-all(f32[16,64,128]{2,1,0:T(8,128)S(1)} %broadcast_in_dim.13), channel_id=1, replica_groups=mesh['users'=32,'items'=16] {'items'}, dimensions={0} | all-to-all | bytes 1048576 | tf_op jit(solution)/shard_map/all_to_all | solution.py:12
  23.8 1.6 %broadcast_in_dim.14 = f32[32,32,128]{2,1,0:T(8,128)} broadcast(f32[32,128]{1,0:T(8,128)} %param.13), dimensions={1,2} | broadcast | bytes 540672 | tf_op jit(solution)/shard_map/broadcast_in_dim | solution.py:13
  25.4 13.3 %all-to-all-start.1 = ((f32[32,32,128]{2,1,0:T(8,128)}), f32[32,32,128]{2,1,0:T(8,128)S(1)}, u32[]{:S(2)}, u32[]{:S(2)}) async-start(f32[32,32,128]{2,1,0:T(8,128)} %broadcast_in_dim.14), calls=%async_computation.1 | async-start | bytes 1048576 | tf_op jit(solution)/shard_map/all_to_all | solution.py:12
  38.7 0.0 copy-start.6
  38.7 5.4 %copy.21 = s32[1024,1024]{0,1:T(8,128)} copy(s32[1024,1024]{1,0:T(8,128)} %param.8) | data formatting | bytes 8388608 | tf_op args[0]
  44.1 17.2 %all-to-all-done.1 = f32[32,32,128]{2,1,0:T(8,128)S(1)} async-done(((f32[32,32,128]{2,1,0:T(8,128)}), f32[32,32,128]{2,1,0:T(8,128)S(1)}, u32[]{:S(2)}, u32[]{:S(2)}) %all-to-all-start.1) | async-done | bytes 524320 | tf_op jit(solution)/shard_map/all_to_all | solution.py:12
  61.3 0.0 copy-done.6
  61.3 8.3 %multiply_reduce_fusion = (f32[1024]{0:T(1024)S(1)}, f32[1024,1024]{0,1:T(8,128)}) fusion(f32[1024,128]{1,0:T(8,128)S(1)} %bitcast.19, f32[1024,128]{1,0:T(8,128)S(1)} %bitcast.20, s32[1024,1024]{0,1:T(8,128)} %copy.21, f32[1024]{0:T(1024)S(1)} %copy-done.6), kind=kOutput, calls=%fused_computation | convolution fusion | flops 1621097472 | bytes 9445376 | tf_op jit(solution)/shard_map/dot_general | solution.py:52
  69.6 0.7 broadcast_in_dim.15
  70.2 4.4 %all-to-all-start.3 = ((f32[16,1,1024]{2,1,0:T(1,128)}), f32[16,1,1024]{2,1,0:T(1,128)S(1)}, u32[]{:S(2)}, u32[]{:S(2)}) async-start(f32[16,1,1024]{2,1,0:T(1,128)} %broadcast_in_dim.15), calls=%async_computation.3 | async-start | bytes 131072 | tf_op jit(solution)/shard_map/all_to_all | solution.py:12
  74.6 5.4 %copy.23 = f32[1024,1024]{1,0:T(8,128)} copy(f32[1024,1024]{0,1:T(8,128)} %get-tuple-element.9) | data formatting | bytes 8388608 | tf_op jit(solution)/shard_map/mul | solution.py:61
  80.0 6.4 %fusion = f32[16,64,128]{2,1,0:T(8,128)} fusion(f32[16,64,1024]{2,1,0:T(8,128)} %bitcast.18, f32[1024,128,1]{1,0,2:T(8,128)S(1)} %bitcast.21), kind=kOutput, calls=%fused_computation.10 | convolution fusion | flops 1610612736 | bytes 5242880 | tf_op jit(solution)/shard_map/dot_general | solution.py:63
  86.5 0.0 all-to-all-done.3
  86.5 7.5 %all-to-all-start.2 = ((f32[16,64,128]{2,1,0:T(8,128)}), f32[16,64,128]{2,1,0:T(8,128)S(1)}, u32[]{:S(2)}, u32[]{:S(2)}) async-start(f32[16,64,128]{2,1,0:T(8,128)} %fusion), calls=%async_computation.2 | async-start | bytes 1048576 | tf_op jit(solution)/shard_map/all_to_all | solution.py:41
  94.0 0.0 copy-start.2
  94.0 0.2 multiply_reduce_fusion.1
  94.2 0.1 reduce_sum.51
  94.3 0.1 reduce_sum.49
  94.3 0.0 copy-done.5
  94.4 0.1 mul.83
  94.4 0.2 broadcast_multiply_fusion
  94.6 6.4 %fusion.1 = f32[32,32,128]{2,1,0:T(8,128)} fusion(f32[32,32,1024]{2,1,0:T(8,128)} %bitcast.17, f32[1024,128,1]{1,0,2:T(8,128)S(1)} %bitcast.22), kind=kOutput, calls=%fused_computation.11 | convolution fusion | flops 1610612736 | bytes 5242880 | tf_op jit(solution)/shard_map/dot_general | solution.py:75
  101.0 6.5 %all-to-all-done.2 = f32[16,64,128]{2,1,0:T(8,128)S(1)} async-done(((f32[16,64,128]{2,1,0:T(8,128)}), f32[16,64,128]{2,1,0:T(8,128)S(1)}, u32[]{:S(2)}, u32[]{:S(2)}) %all-to-all-start.2) | async-done | bytes 524320 | tf_op jit(solution)/shard_map/all_to_all | solution.py:41
  107.6 3.9 %all-to-all-start.4 = ((f32[32,32,128]{2,1,0:T(8,128)}), f32[32,32,128]{2,1,0:T(8,128)S(1)}, u32[]{:S(2)}, u32[]{:S(2)}) async-start(f32[32,32,128]{2,1,0:T(8,128)} %fusion.1), calls=%async_computation.4 | async-start | bytes 1048576 | tf_op jit(solution)/shard_map/all_to_all | solution.py:41
  111.5 0.0 copy-done
  111.6 0.6 multiply_subtract_fusion
  112.2 21.7 %all-to-all-done.4 = f32[32,32,128]{2,1,0:T(8,128)S(1)} async-done(((f32[32,32,128]{2,1,0:T(8,128)}), f32[32,32,128]{2,1,0:T(8,128)S(1)}, u32[]{:S(2)}, u32[]{:S(2)}) %all-to-all-start.4) | async-done | bytes 524320 | tf_op jit(solution)/shard_map/all_to_all | solution.py:41
  133.9 0.0 copy-done.1
  133.9 0.0 copy-done.3
  134.0 0.0 copy-done.4
  134.0 0.6 multiply_subtract_fusion.1
  (9 shorter events, 0.1 us)
Async XLA Ops:
  25.4 35.9 %all-to-all-start.1 = ((f32[32,32,128]{2,1,0:T(8,128)}), f32[32,32,128]{2,1,0:T(8,128)S(1)}, u32[]{:S(2)}, u32[]{:S(2)}) async-start(f32[32,32,128]{2,1,0:T(8,128)} %broadcast_in_dim.14), calls=%async_computation.1 | async-start | bytes 1048576 | tf_op jit(solution)/shard_map/all_to_all | solution.py:12
  38.7 22.6 %copy-start.6 = (f32[1024]{0:T(1024)S(1)}, f32[1024]{0:T(1024)}, u32[]{:S(2)}) copy-start(f32[1024]{0:T(1024)} %param.9) | copy-start | bytes 12292
  70.2 16.2 %all-to-all-start.3 = ((f32[16,1,1024]{2,1,0:T(1,128)}), f32[16,1,1024]{2,1,0:T(1,128)S(1)}, u32[]{:S(2)}, u32[]{:S(2)}) async-start(f32[16,1,1024]{2,1,0:T(1,128)} %broadcast_in_dim.15), calls=%async_computation.3 | async-start | bytes 131072 | tf_op jit(solution)/shard_map/all_to_all | solution.py:12
  80.0 14.3 %copy-start.5 = (s32[1024]{0:T(1024)S(1)}, s32[1024]{0:T(1024)}, u32[]{:S(2)}) copy-start(s32[1024]{0:T(1024)} %param.10) | copy-start | bytes 12292
  86.5 21.1 %all-to-all-start.2 = ((f32[16,64,128]{2,1,0:T(8,128)}), f32[16,64,128]{2,1,0:T(8,128)S(1)}, u32[]{:S(2)}, u32[]{:S(2)}) async-start(f32[16,64,128]{2,1,0:T(8,128)} %fusion), calls=%async_computation.2 | async-start | bytes 1048576 | tf_op jit(solution)/shard_map/all_to_all | solution.py:41
  94.0 17.6 %copy-start = (f32[64,128]{1,0:T(8,128)S(1)}, f32[64,128]{1,0:T(8,128)}, u32[]{:S(2)}) copy-start(f32[64,128]{1,0:T(8,128)} %param.11) | copy-start | bytes 98308
  94.0 17.6 %copy-start.2 = (f32[64,128]{1,0:T(8,128)S(1)}, f32[64,128]{1,0:T(8,128)}, u32[]{:S(2)}) copy-start(f32[64,128]{1,0:T(8,128)} %param.12) | copy-start | bytes 98308
  94.4 39.5 %copy-start.1 = (f32[32,128]{1,0:T(8,128)S(1)}, f32[32,128]{1,0:T(8,128)}, u32[]{:S(2)}) copy-start(f32[32,128]{1,0:T(8,128)} %param.13) | copy-start | bytes 49156
  94.4 39.5 %copy-start.3 = (s32[32,128]{1,0:T(8,128)S(1)}, s32[32,128]{1,0:T(8,128)}, u32[]{:S(2)}) copy-start(s32[32,128]{1,0:T(8,128)} %param.15) | copy-start | bytes 49156
  94.4 39.5 %copy-start.4 = (f32[32,128]{1,0:T(8,128)S(1)}, f32[32,128]{1,0:T(8,128)}, u32[]{:S(2)}) copy-start(f32[32,128]{1,0:T(8,128)} %param.14) | copy-start | bytes 49156
  107.6 26.3 %all-to-all-start.4 = ((f32[32,32,128]{2,1,0:T(8,128)}), f32[32,32,128]{2,1,0:T(8,128)S(1)}, u32[]{:S(2)}, u32[]{:S(2)}) async-start(f32[32,32,128]{2,1,0:T(8,128)} %fusion.1), calls=%async_computation.4 | async-start | bytes 1048576 | tf_op jit(solution)/shard_map/all_to_all | solution.py:41
where the time goes:
time: 135 us
  waiting for transfers between devices  45.4 us (34%)
  starting transfers between devices  29.1 us (22%)
  blocking collectives  22.4 us (17%)
  matrix products  21.1 us (16%)
  local copies, waits for them, and re-layouts  13.9 us (10%)
  other arithmetic  1.81 us (1%)
    all_to_all x2, waiting for transfers between devices, sent_and_summed(): tiles = lax.all_to_all(cut_along(value, dim, peers), axis, 0, 0, tiled=True)  28.2 us
    all_to_all x1, blocking collectives, from_everyone(): lax.all_to_all(jnp.broadcast_to(value[None], (peers, *value.shape)), axis...  22.4 us
    all_to_all x2, starting transfers between devices, from_everyone(): lax.all_to_all(jnp.broadcast_to(value[None], (peers, *value.shape)), axis...  17.7 us
    all_to_all x2, waiting for transfers between devices, from_everyone(): lax.all_to_all(jnp.broadcast_to(value[None], (peers, *value.shape)), axis...  17.2 us
    all_to_all x2, starting transfers between devices, sent_and_summed(): tiles = lax.all_to_all(cut_along(value, dim, peers), axis, 0, 0, tiled=True)  11.4 us
    dot_general x1, matrix products, local(): lax.dot_general(user_rows, portion, (((1,), (1,)), ((), ())), precision=p...  8.3 us
    dot_general x1, matrix products, local(): jnp.dot(weighted, portion, precision=precise, preferred_element_type=jnp....  6.44 us
    dot_general x1, matrix products, local(): lax.dot_general(weighted, scaled, (((0,), (0,)), ((), ())), precision=pre...  6.4 us
  transfers between devices with their start and end apart: 4, of which 3 were waited for; matrix products, arithmetic and copies ran while one was open for 18% of the time, Pallas kernels for 0%

commit v1 on v0

v1 whole, which is shorter than its diff:
```python
import jax
import jax.numpy as jnp
from jax import lax
from jax.experimental import pallas as pl
from jax.experimental.pallas import tpu as pltpu
from jax.sharding import Mesh, PartitionSpec as P

noise_step = 0.05
learn_rate = 0.5
lanes = 128
f32 = jnp.float32
bf16 = jnp.bfloat16

names = ("z", "half", "core", "run", "x")
sizes = (8, 2, 2, 4, 4)
user_axes = names[:3]
item_axes = names[3:]
chip_axes = names[:2]

whole = pl.BlockSpec(memory_space=pltpu.VMEM)


def halves(value):
    high = value.astype(bf16)
    return high, (value - high.astype(f32)).astype(bf16)


def product(left, right):
    return jnp.dot(left, right, preferred_element_type=f32)


def cost(flops):
    return pl.CostEstimate(flops=flops, bytes_accessed=1 << 20, transcendentals=0)


def block_kernel(
    user_ref, item_ref, far_ref, rate_ref, high_ref, low_ref, sent_ref, turned_ref, norm_ref, pair_ref, rest_ref, tall_ref, prefs_ref, ready
):
    parts, steps, piece, width = user_ref.shape
    users, items = prefs_ref.shape
    rows = parts * piece
    tile = 2 * lanes
    blocks = [slice(step * rows, (step + 1) * rows) for step in range(steps)]
    copies = [pltpu.make_async_copy(far_ref.at[span], prefs_ref.at[span], ready.at[step]) for step, span in enumerate(blocks)]
    for copy in copies:
        copy.start()
    cores, _, bit, _ = item_ref.shape
    per = lanes // (cores * bit)
    for part in range(items // lanes):
        place = slice(part * lanes, (part + 1) * lanes)
        together = [item_ref[core, part * per + line] for line in range(per) for core in range(cores)]
        value = jnp.concatenate(together, axis=0)
        high, low = halves(value)
        tall_ref[place, :width] = high
        tall_ref[place, width:] = low
        high, low = halves(value.T)
        pair_ref[:width, place] = high
        pair_ref[width:, place] = high
        rest_ref[:, place] = low
    for step, span in enumerate(blocks):
        user = user_ref[:, step].reshape(rows, width)
        user_high, user_low = halves(user)
        both = jnp.concatenate([user_high, user_low], axis=1)
        squares = jnp.zeros((rows, lanes), f32)
        copies[step].wait()
        for part in range(items // tile):
            place = slice(part * tile, (part + 1) * tile)
            predicted = product(both, pair_ref[:, place]) + product(user_high, rest_ref[:, place])
            level = prefs_ref[span, place].astype(f32)
            confidence = 2.0 + 2.0 * rate_ref[:, place] * level
            weighted = confidence * (predicted - jnp.where(level > 0, 1.0, 0.0))
            high_ref[span, place], low_ref[span, place] = halves(weighted)
            square = weighted * weighted
            squares = squares + square[:, :lanes] + square[:, lanes:]
        wide = product(high_ref[span, :], tall_ref[...])
        gradient = wide[:, :width] + wide[:, width:] + product(low_ref[span, :], tall_ref[:, :width])
        for part in range(parts):
            sent_ref[part, step * piece : (step + 1) * piece, :] = gradient[part * piece : (part + 1) * piece, :]
        for part in range(rows // lanes):
            place = slice(part * lanes, (part + 1) * lanes)
            row = step * (rows // lanes) + part
            turned = user[place, :].T
            turned_ref[:, row * lanes : (row + 1) * lanes] = turned
            norm_ref[row : row + 1, :] = jnp.sum(turned * turned, axis=0, keepdims=True)
            total = jnp.sum(squares[place, :].T, axis=0, keepdims=True)
            for other in range(parts):
                sent_ref[other, steps * piece + row : steps * piece + row + 1, :] = total


def block(user_rows, item_rows, prefs, rate):
    parts, steps, piece, width = user_rows.shape
    users, items = prefs.shape
    groups = users // lanes
    return pl.pallas_call(
        block_kernel,
        in_specs=[whole, whole, pl.BlockSpec(memory_space=pltpu.HBM), whole],
        out_specs=[whole] * 5,
        out_shape=[
            jax.ShapeDtypeStruct((users, items), bf16),
            jax.ShapeDtypeStruct((users, items), bf16),
            jax.ShapeDtypeStruct((parts, steps * piece + groups, width), f32),
            jax.ShapeDtypeStruct((width, users), f32),
            jax.ShapeDtypeStruct((groups, lanes), f32),
        ],
        scratch_shapes=[
            pltpu.VMEM((2 * width, items), bf16),
            pltpu.VMEM((width, items), bf16),
            pltpu.VMEM((items, 2 * width), bf16),
            pltpu.VMEM((users, items), jnp.int32),
            pltpu.SemaphoreType.DMA((steps,)),
        ],
        compiler_params=pltpu.CompilerParams(vmem_limit_bytes=32 << 20),
        cost_estimate=cost(12 * users * items * width),
        name="block",
    )(user_rows, item_rows, pltpu.with_memory_space_constraint(prefs, pltpu.HBM), rate)


def relay_kernel(tiles_ref, out_ref):
    runs, rows, width = out_ref.shape
    piece = (tiles_ref.shape[1] - rows) // (runs - 1)
    summed = jnp.sum(tiles_ref[...], axis=0)
    for run in range(runs):
        out_ref[run, :piece, :] = summed[run * piece : (run + 1) * piece]
        out_ref[run, piece:, :] = summed[runs * piece :]


def relay(tiles, runs, groups):
    rows = tiles.shape[1] - groups
    return pl.pallas_call(
        relay_kernel,
        in_specs=[whole],
        out_specs=whole,
        out_shape=jax.ShapeDtypeStruct((runs, rows // runs + groups, lanes), f32),
        compiler_params=pltpu.CompilerParams(vmem_limit_bytes=8 << 20),
        cost_estimate=cost(1 << 20),
        name="relay",
    )(tiles)


def item_kernel(bound_scale, slab_ref, norm_ref, clip_ref, turned_ref, high_ref, low_ref, keep_ref, give_ref, pair_ref):
    width, users = turned_ref.shape
    items = high_ref.shape[1]
    groups = norm_ref.shape[0]
    bit = keep_ref.shape[1]
    tile = 2 * lanes
    first = lax.axis_index("core") == 0
    total = jnp.sum(slab_ref[:, slab_ref.shape[1] - groups :, :], axis=0)
    bound = clip_ref[...].astype(f32) * bound_scale
    factor = jnp.minimum(1.0, bound / jnp.sqrt(total * norm_ref[...] + 1e-06))
    for part in range(users // lanes):
        place = slice(part * lanes, (part + 1) * lanes)
        pair_ref[:width, place], pair_ref[width:, place] = halves(turned_ref[:, place] * factor[part : part + 1, :])
    for part in range(items // tile):
        place = slice(part * tile, (part + 1) * tile)
        tall = product(pair_ref[...], high_ref[:, place])
        summed = tall[:width] + tall[width:] + product(pair_ref[:width, :], low_ref[:, place])
        for inner in range(tile // lanes):
            rows = summed[:, inner * lanes : (inner + 1) * lanes].T
            for piece in range(lanes // (2 * bit)):
                index = (part * tile + inner * lanes) // (2 * bit) + piece
                even = rows[2 * piece * bit : (2 * piece + 1) * bit, :]
                odd = rows[(2 * piece + 1) * bit : (2 * piece + 2) * bit, :]
                keep_ref[index] = jnp.where(first, even, odd)
                give_ref[index] = jnp.where(first, odd, even)


def item_gradients(bound_scale, slab, norm, clip, turned, high, low, bit):
    users, items = high.shape
    width = turned.shape[0]

    def body(*refs):
        item_kernel(bound_scale, *refs)

    return pl.pallas_call(
        body,
        in_specs=[whole] * 6,
        out_specs=[whole] * 2,
        out_shape=[jax.ShapeDtypeStruct((items // (2 * bit), bit, width), f32)] * 2,
        scratch_shapes=[pltpu.VMEM((2 * width, users), bf16)],
        compiler_params=pltpu.CompilerParams(vmem_limit_bytes=24 << 20),
        cost_estimate=cost(6 * users * items * width),
        name="item_gradients",
    )(slab, norm, clip, turned, high, low)


def join_kernel(keep_ref, both_ref, out_ref):
    out_ref[...] = keep_ref[...] + both_ref[1 - lax.axis_index("core")]


def join(keep, both):
    return pl.pallas_call(
        join_kernel,
        in_specs=[whole] * 2,
        out_specs=whole,
        out_shape=jax.ShapeDtypeStruct(keep.shape, f32),
        compiler_params=pltpu.CompilerParams(vmem_limit_bytes=8 << 20),
        cost_estimate=cost(1 << 20),
        name="join",
    )(keep, both)


def step_of(emb, acc, gradient):
    new_acc = acc + gradient * gradient
    return emb - learn_rate * gradient / jnp.sqrt(new_acc), new_acc


def user_kernel(slab_ref, emb_ref, acc_ref, emb_out, acc_out):
    gradient = jnp.sum(slab_ref[:, : emb_ref.shape[0], :], axis=0)
    emb_out[...], acc_out[...] = step_of(emb_ref[...], acc_ref[...], gradient)


def last_kernel(tiles_ref, emb_ref, acc_ref, noise_ref, emb_out, acc_out):
    gradient = jnp.sum(tiles_ref[...], axis=0) + noise_step * noise_ref[...].astype(f32)
    emb_out[...], acc_out[...] = step_of(emb_ref[...], acc_ref[...], gradient)


def finish(body, name, tiles, emb, *rest):
    result = jax.ShapeDtypeStruct(emb.shape, f32)
    return pl.pallas_call(
        body,
        in_specs=[whole] * (2 + len(rest)),
        out_specs=[whole] * 2,
        out_shape=[result] * 2,
        compiler_params=pltpu.CompilerParams(vmem_limit_bytes=8 << 20),
        cost_estimate=cost(1 << 24),
        name=name,
    )(tiles, emb, *rest)


def exchange(value, axis):
    return lax.all_to_all(value, axis, 0, 0, tiled=True)


def from_everyone(value, axis):
    return exchange(jnp.broadcast_to(value[None], (lax.axis_size(axis), *value.shape)), axis)


def local(prefs, item_weight, clip_units, user_emb, user_acc, item_emb, item_acc, noise):
    users, items = prefs.shape
    piece, width = user_emb.shape
    bit = item_emb.shape[0]
    groups = users // lanes
    bound_scale = 0.001 * (items * lax.axis_size(item_axes) * width) ** 0.5
    user_run = from_everyone(user_emb, "run")
    item_pair = lax.all_gather(item_emb, "half")
    item_line = from_everyone(item_pair, "z").reshape(-1, bit, width)
    user_rows = lax.all_gather(user_run, "x")
    item_rows = lax.all_gather(item_line, "core")
    high, low, sent, turned, norm = block(user_rows, item_rows, prefs, item_weight.reshape(1, items))
    slab = exchange(relay(exchange(sent, "x"), lax.axis_size("run"), groups), "run")
    keep, give = item_gradients(bound_scale, slab, norm, clip_units.reshape(groups, lanes), turned, high, low, bit)
    tiles = exchange(join(keep, lax.all_gather(give, "core")), chip_axes)
    users_new = finish(user_kernel, "finish_users", slab, user_emb, user_acc)
    items_new = finish(last_kernel, "finish_items", tiles, item_emb, item_acc, noise)
    return (*users_new, *items_new)


def solution(mesh):
    fine = Mesh(mesh.devices.reshape(sizes), names)
    by_user = P(user_axes + item_axes, None)
    by_item = P(item_axes + user_axes, None)
    return jax.shard_map(
        local,
        mesh=fine,
        in_specs=(P(user_axes, item_axes), P(item_axes), P(user_axes), by_user, by_user, by_item, by_item, by_item),
        out_specs=(by_user, by_user, by_item, by_item),
        check_vma=False,
    )
```

time: 135 us -> 104 us (0.77)
  waiting for transfers between devices: 45.4 us -> 15.9 us
  blocking collectives: 22.4 us -> 49.5 us
  matrix products: 21.1 us -> 0 us
  local copies, waits for them, and re-layouts: 13.9 us -> 2.19 us
  Pallas kernels: 0 us -> 8.35 us
  starting transfers between devices: 29.1 us -> 26.9 us
  other arithmetic: 1.81 us -> 0 us
    all_to_all x4 -> x3, waiting for transfers between devices: 45.4 us -> 15.9 us  [exchange(): return lax.all_to_all(value, axis, 0, 0, tiled=True)]
    all_gather x0 -> x4, blocking collectives: none -> 26.7 us  [the longest x1 13.7 us: local(): user_rows = lax.all_gather(user_run, 'x')]
    dot_general x3 -> x0, matrix products: 21.1 us -> none  [the longest x1 8.3 us: local(): lax.dot_general(user_rows, portion, (((1,), (1,)), ((), ())), precision=p...]
    pallas_call x0 -> x6, Pallas kernels: none -> 8.35 us  [the longest x1 5.15 us: block(): pl.pallas_call(block_kernel, in_specs=[whole, whole, pl.BlockSpec(memory_...]
    mul x2 -> x0, local copies, waits for them, and re-layouts: 5.44 us -> none  [the longest x1 5.37 us: local(): weighted = -2.0 * confidence * (target - predicted)]
    unnamed x15 -> x14, local copies, waits for them, and re-layouts: 5.4 us -> 0.04 us
    all_to_all x4 -> x3, starting transfers between devices: 29.1 us -> 26.9 us  [exchange(): return lax.all_to_all(value, axis, 0, 0, tiled=True)]
    broadcast_in_dim x3 -> x2, local copies, waits for them, and re-layouts: 3.03 us -> 2.15 us  [from_everyone(): jnp.broadcast_to(value[None], (lax.axis_size(axis), *value.shape))]
  transfers between devices with their start and end apart: 4 -> 3, of which waited for: 3 -> 1; matrix products, arithmetic and copies ran while one was open for 18% -> 0% of each run, Pallas kernels for 0% -> 1%
where the time goes in v1:
time: 104 us
  blocking collectives  49.5 us (48%)
  starting transfers between devices  26.9 us (26%)
  waiting for transfers between devices  15.9 us (15%)
  Pallas kernels  8.35 us (8%)
  local copies, waits for them, and re-layouts  2.19 us (2%)
    all_to_all x3, starting transfers between devices, exchange(): return lax.all_to_all(value, axis, 0, 0, tiled=True)  26.9 us
    all_to_all x2, blocking collectives, exchange(): return lax.all_to_all(value, axis, 0, 0, tiled=True)  22.8 us
    all_to_all x3, waiting for transfers between devices, exchange(): return lax.all_to_all(value, axis, 0, 0, tiled=True)  15.9 us
    all_gather x1, blocking collectives, local(): user_rows = lax.all_gather(user_run, 'x')  13.7 us
    all_gather x1, blocking collectives, local(): item_pair = lax.all_gather(item_emb, 'half')  8.51 us
    pallas_call x1, Pallas kernels, block(): pl.pallas_call(block_kernel, in_specs=[whole, whole, pl.BlockSpec(memory_...  5.15 us
    all_gather x1, blocking collectives, local(): tiles = exchange(join(keep, lax.all_gather(give, 'core')), chip_axes)  2.31 us
    all_gather x1, blocking collectives, local(): item_rows = lax.all_gather(item_line, 'core')  2.17 us
  transfers between devices with their start and end apart: 3, of which 1 were waited for; matrix products, arithmetic and copies ran while one was open for 0% of the time, Pallas kernels for 1%

profile of v1, /device:TPU:8, one launch (start us, length us, event | category | flops | bytes accessed | tf_op | source)
XLA Modules:
  0.0 103.5 jit_solution(3106485615566841739)
XLA Ops:
  0.6 0.0 copy-start.6
  0.6 1.4 %broadcast_in_dim.4 = f32[4,64,128]{2,1,0:T(8,128)} broadcast(f32[64,128]{1,0:T(8,128)} %emb_ref.2), dimensions={1,2} | broadcast | bytes 163840 | tf_op jit(solution)/shard_map/broadcast_in_dim | solution.py:235
  2.1 9.1 %all-to-all-start = ((f32[4,64,128]{2,1,0:T(8,128)}), f32[4,64,128]{2,1,0:T(8,128)S(1)}, u32[]{:S(2)}, u32[]{:S(2)}) async-start(f32[4,64,128]{2,1,0:T(8,128)} %broadcast_in_dim.4), calls=%async_computation | async-start | bytes 262144 | tf_op jit(solution)/shard_map/all_to_all | solution.py:231
  11.2 8.5 %all-gather.1 = f32[64,128]{1,0:T(8,128)S(1)} all-gather(f32[32,128]{1,0:T(8,128)} %emb_ref.3), channel_id=3, replica_groups=mesh['z'=8,'half'=2,'core'=2,'run'=4,'x'=4] {'half'}, dimensions={0}, use_global_device_ids=true | all-gather | bytes 49152 | tf_op jit(solution)/shard_map/all_gather | solution.py:245
  19.7 0.0 all-to-all-done
  19.7 0.7 broadcast_in_dim.5
  20.4 6.8 %all-to-all-start.1 = ((f32[8,2,32,128]{3,2,1,0:T(8,128)}), f32[8,2,32,128]{3,2,1,0:T(8,128)S(1)}, u32[]{:S(2)}, u32[]{:S(2)}) async-start(f32[8,2,32,128]{3,2,1,0:T(8,128)} %broadcast_in_dim.5), calls=%async_computation.1 | async-start | bytes 524288 | tf_op jit(solution)/shard_map/all_to_all | solution.py:231
  27.2 13.7 %all-gather = f32[16,64,128]{2,1,0:T(8,128)S(1)} all-gather(f32[4,64,128]{2,1,0:T(8,128)S(1)} %all-to-all-done), channel_id=2, replica_groups=mesh['z'=8,'half'=2,'core'=2,'run'=4,'x'=4] {'x'}, dimensions={0}, use_global_device_ids=true | all-gather | bytes 655360 | tf_op jit(solution)/shard_map/all_gather | solution.py:247
  40.9 0.0 all-to-all-done.1
  40.9 2.2 %all_gather.25.item_ref = f32[2,16,32,128]{3,2,1,0:T(8,128)S(1)} all-gather(f32[1,16,32,128]{3,2,1,0:T(8,128)S(1)} %bitcast.10), channel_id=1, replica_groups=mesh['z'=8,'half'=2,'core'=2,'run'=4,'x'=4] {'core'}, dimensions={0}, use_global_device_ids=true | all-gather | bytes 786432 | tf_op jit(solution)/shard_map/all_gather | solution.py:248
  43.1 0.0 copy-done.6
  43.1 5.2 %block.1 = (bf16[1024,1024]{1,0:T(8,128)(2,1)S(1)}, bf16[1024,1024]{1,0:T(8,128)(2,1)S(1)}, f32[4,264,128]{2,1,0:T(8,128)S(1)}, f32[128,1024]{1,0:T(8,128)S(1)}, f32[8,128]{1,0:T(8,128)S(1)}) custom-call(f32[4,4,64,128]{3,2,1,0:T(8,128)S(1)} %bitcast.7, f32[2,16,32,128]{3,2,1,0:T(8,128)S(1)} %all_gather.25.item_ref, s32[1024,1024]{1,0:T(8,128)} %far_ref.1, ...), custom_call_target="tpu_custom_call" | custom-call | flops 1610612736 | bytes 1048576 | tf_op jit(solution)/shard_map/block/pallas_call | solution.py:94
  48.2 12.8 %all_to_all.25.tiles_ref = f32[4,264,128]{2,1,0:T(8,128)S(1)} all-to-all(f32[4,264,128]{2,1,0:T(8,128)S(1)} %get-tuple-element.15), channel_id=1, replica_groups=mesh['z'=8,'half'=2,'core'=2,'run'=4,'x'=4] {'x'}, dimensions={0} | all-to-all | bytes 1081344 | tf_op jit(solution)/shard_map/all_to_all | solution.py:231
  61.1 10.0 %all_to_all.26.slab_ref.refs_0_ = f32[4,72,128]{2,1,0:T(8,128)S(1)} all-to-all(f32[4,72,128]{2,1,0:T(8,128)S(1)} %relay.1), channel_id=1, replica_groups=mesh['z'=8,'half'=2,'core'=2,'run'=4,'x'=4] {'run'}, dimensions={0} | all-to-all | bytes 294912 | tf_op jit(solution)/shard_map/all_to_all | solution.py:231
  71.1 0.0 copy-done.5
  71.1 1.1 %item_gradients.1 = (f32[16,32,128]{2,1,0:T(8,128)S(1)}, f32[16,32,128]{2,1,0:T(8,128)S(1)}) custom-call(f32[4,72,128]{2,1,0:T(8,128)S(1)} %all_to_all.26.slab_ref.refs_0_, f32[8,128]{1,0:T(8,128)S(1)} %get-tuple-element.18.refs_1_, s32[8,128]{1,0:T(8,128)S(1)} %bitcast.8, f32[128,1024]{1,0:T(8,128)S(1)} %get-tuple-element.19.refs_3_, ...), custom_call_target="tpu_custom_call" | custom-call | flops 805306368 | bytes 1048576 | tf_op jit(solution)/shard_map/item_gradients/pallas_call | solution.py:174
  72.2 0.0 copy-start
  72.2 0.0 copy-start.2
  72.2 0.0 copy-start.1
  72.2 0.0 copy-start.3
  72.2 0.0 copy-start.4
  72.3 2.3 %all-gather.2 = f32[32,32,128]{2,1,0:T(8,128)S(1)} all-gather(f32[16,32,128]{2,1,0:T(8,128)S(1)} %get-tuple-element.23), channel_id=4, replica_groups=mesh['z'=8,'half'=2,'core'=2,'run'=4,'x'=4] {'core'}, dimensions={0}, use_global_device_ids=true | all-gather | bytes 786432 | tf_op jit(solution)/shard_map/all_gather | solution.py:252
  74.6 0.7 join.1
  75.3 11.0 %all-to-all-start.4 = ((f32[16,32,128]{2,1,0:T(8,128)}), f32[16,32,128]{2,1,0:T(8,128)S(1)}, u32[]{:S(2)}, u32[]{:S(2)}) async-start(f32[16,32,128]{2,1,0:T(8,128)} %join.1), calls=%async_computation.4 | async-start | bytes 524288 | tf_op jit(solution)/shard_map/all_to_all | solution.py:231
  86.3 0.0 copy-done
  86.3 0.0 copy-done.2
  86.3 0.7 finish_users.1
  87.0 15.9 %all-to-all-done.4.tiles_ref = f32[16,32,128]{2,1,0:T(8,128)S(1)} async-done(((f32[16,32,128]{2,1,0:T(8,128)}), f32[16,32,128]{2,1,0:T(8,128)S(1)}, u32[]{:S(2)}, u32[]{:S(2)}) %all-to-all-start.4) | async-done | bytes 262176 | tf_op jit(solution)/shard_map/all_to_all | solution.py:231
  102.9 0.0 copy-done.1
  102.9 0.0 copy-done.3
  102.9 0.0 copy-done.4
  102.9 0.7 finish_items.1
  (2 shorter events, 0.0 us)
Async XLA Ops:
  0.6 42.4 %copy-start.6 = (f32[1024]{0:T(1024)S(1)}, f32[1024]{0:T(1024)}, u32[]{:S(2)}) copy-start(f32[1024]{0:T(1024)} %param.9) | copy-start | bytes 12292
  2.1 17.6 %all-to-all-start = ((f32[4,64,128]{2,1,0:T(8,128)}), f32[4,64,128]{2,1,0:T(8,128)S(1)}, u32[]{:S(2)}, u32[]{:S(2)}) async-start(f32[4,64,128]{2,1,0:T(8,128)} %broadcast_in_dim.4), calls=%async_computation | async-start | bytes 262144 | tf_op jit(solution)/shard_map/all_to_all | solution.py:231
  20.4 20.5 %all-to-all-start.1 = ((f32[8,2,32,128]{3,2,1,0:T(8,128)}), f32[8,2,32,128]{3,2,1,0:T(8,128)S(1)}, u32[]{:S(2)}, u32[]{:S(2)}) async-start(f32[8,2,32,128]{3,2,1,0:T(8,128)} %broadcast_in_dim.5), calls=%async_computation.1 | async-start | bytes 524288 | tf_op jit(solution)/shard_map/all_to_all | solution.py:231
  43.1 28.0 %copy-start.5 = (s32[1024]{0:T(1024)S(1)}, s32[1024]{0:T(1024)}, u32[]{:S(2)}) copy-start(s32[1024]{0:T(1024)} %param.10) | copy-start | bytes 12292
  72.2 14.1 %copy-start = (f32[64,128]{1,0:T(8,128)S(1)}, f32[64,128]{1,0:T(8,128)}, u32[]{:S(2)}) copy-start(f32[64,128]{1,0:T(8,128)} %emb_ref.2) | copy-start | bytes 98308
  72.2 14.1 %copy-start.2 = (f32[64,128]{1,0:T(8,128)S(1)}, f32[64,128]{1,0:T(8,128)}, u32[]{:S(2)}) copy-start(f32[64,128]{1,0:T(8,128)} %acc_ref.2) | copy-start | bytes 98308
  72.2 30.7 %copy-start.1 = (f32[32,128]{1,0:T(8,128)S(1)}, f32[32,128]{1,0:T(8,128)}, u32[]{:S(2)}) copy-start(f32[32,128]{1,0:T(8,128)} %emb_ref.3) | copy-start | bytes 49156
  72.2 30.6 %copy-start.3 = (f32[32,128]{1,0:T(8,128)S(1)}, f32[32,128]{1,0:T(8,128)}, u32[]{:S(2)}) copy-start(f32[32,128]{1,0:T(8,128)} %acc_ref.3) | copy-start | bytes 49156
  72.2 30.6 %copy-start.4 = (s32[32,128]{1,0:T(8,128)S(1)}, s32[32,128]{1,0:T(8,128)}, u32[]{:S(2)}) copy-start(s32[32,128]{1,0:T(8,128)} %noise_ref.1) | copy-start | bytes 49156
  75.3 27.6 %all-to-all-start.4 = ((f32[16,32,128]{2,1,0:T(8,128)}), f32[16,32,128]{2,1,0:T(8,128)S(1)}, u32[]{:S(2)}, u32[]{:S(2)}) async-start(f32[16,32,128]{2,1,0:T(8,128)} %join.1), calls=%async_computation.4 | async-start | bytes 524288 | tf_op jit(solution)/shard_map/all_to_all | solution.py:231

commit v2 on v1

v2 whole, which is shorter than its diff:
```python
import jax
import jax.numpy as jnp
from jax import lax
from jax.experimental import pallas as pl
from jax.experimental.pallas import tpu as pltpu
from jax.sharding import Mesh, PartitionSpec as P

noise_step = 0.05
learn_rate = 0.5
lanes = 128
f32 = jnp.float32
bf16 = jnp.bfloat16

names = ("z", "half", "core", "run", "x")
sizes = (8, 2, 2, 4, 4)
user_axes = names[:3]
item_axes = names[3:]

whole = pl.BlockSpec(memory_space=pltpu.VMEM)
far = pl.BlockSpec(memory_space=pltpu.HBM)


def halves(value):
    high = value.astype(bf16)
    return high, (value - high.astype(f32)).astype(bf16)


def product(left, right):
    return jnp.dot(left, right, preferred_element_type=f32)


def cost(flops):
    return pl.CostEstimate(flops=flops, bytes_accessed=1 << 20, transcendentals=0)


def block_kernel(
    own_ref, one_ref, two_ref, three_ref, item_ref, far_ref, far_rate_ref, high_ref, low_ref, sq_ref, turned_ref, norm_ref, *more_refs
):
    *out_refs, pair_ref, rest_ref, tall_ref, prefs_ref, rate_ref, near_ref, user_ref, sum_ref, ready, gone, rated = more_refs
    parts, steps, piece, width = user_ref.shape
    mine = lax.axis_index("x")
    _, items = prefs_ref.shape
    rows = parts * piece
    tile = 2 * lanes
    blocks = [slice(step * rows, (step + 1) * rows) for step in range(steps)]
    copies = [pltpu.make_async_copy(far_ref.at[span], prefs_ref.at[span], ready.at[step]) for step, span in enumerate(blocks)]
    rates = pltpu.make_async_copy(far_rate_ref, rate_ref, rated)
    rates.start()
    for copy in copies:
        copy.start()
    stores = [pltpu.make_async_copy(near_ref.at[span], low_ref.at[span], gone.at[step]) for step, span in enumerate(blocks)]
    for shift, ref in enumerate((own_ref, one_ref, two_ref, three_ref)):
        user_ref[lax.rem(mine + parts - shift, parts)] = ref[...]
    cores, _, bit, _ = item_ref.shape
    per = lanes // (cores * bit)
    for part in range(items // lanes):
        place = slice(part * lanes, (part + 1) * lanes)
        together = [item_ref[core, part * per + line] for line in range(per) for core in range(cores)]
        value = jnp.concatenate(together, axis=0)
        high, low = halves(value)
        tall_ref[place, :width] = high
        tall_ref[place, width:] = low
        high, low = halves(value.T)
        pair_ref[:width, place] = high
        pair_ref[width:, place] = high
        rest_ref[:, place] = low
    for step, span in enumerate(blocks):
        user = user_ref[:, step].reshape(rows, width)
        user_high, user_low = halves(user)
        both = jnp.concatenate([user_high, user_low], axis=1)
        squares = jnp.zeros((rows, lanes), f32)
        if step == 0:
            rates.wait()
        copies[step].wait()
        for part in range(items // tile):
            place = slice(part * tile, (part + 1) * tile)
            predicted = product(both, pair_ref[:, place]) + product(user_high, rest_ref[:, place])
            level = prefs_ref[span, place].astype(f32)
            confidence = 2.0 + 2.0 * rate_ref[:, place] * level
            weighted = confidence * (predicted - jnp.where(level > 0, 1.0, 0.0))
            high_ref[span, place], near_ref[span, place] = halves(weighted)
            square = weighted * weighted
            squares = squares + square[:, :lanes] + square[:, lanes:]
        stores[step].start()
        for part in range(rows // lanes):
            row = step * (rows // lanes) + part
            total = squares[part * lanes : (part + 1) * lanes, :].T
            sq_ref[row : row + 1, :] = jnp.sum(total, axis=0, keepdims=True)
    for step, span in enumerate(blocks):
        user = user_ref[:, step].reshape(rows, width)
        wide = product(high_ref[span, :], tall_ref[...])
        gradient = wide[:, :width] + wide[:, width:] + product(near_ref[span, :], tall_ref[:, :width])
        for part in range(parts):
            sum_ref[part, step * piece : (step + 1) * piece, :] = gradient[part * piece : (part + 1) * piece, :]
        for part in range(rows // lanes):
            row = step * (rows // lanes) + part
            turned = user[part * lanes : (part + 1) * lanes, :].T
            turned_ref[:, row * lanes : (row + 1) * lanes] = turned
            norm_ref[row : row + 1, :] = jnp.sum(turned * turned, axis=0, keepdims=True)
    for shift, out_ref in enumerate(out_refs):
        out_ref[...] = sum_ref[lax.rem(mine + shift, parts)]
    for store in stores:
        store.wait()


def block(user_rows, item_rows, prefs, rate):
    parts = len(user_rows)
    steps, piece, width = user_rows[0].shape
    users, items = prefs.shape
    groups = users // lanes
    return pl.pallas_call(
        block_kernel,
        in_specs=[whole] * (parts + 1) + [far] * 2,
        out_specs=[whole, far] + [whole] * (3 + parts),
        out_shape=[
            jax.ShapeDtypeStruct((users, items), bf16),
            pltpu.HBM((users, items), bf16),
            jax.ShapeDtypeStruct((groups, lanes), f32),
            jax.ShapeDtypeStruct((width, users), f32),
            jax.ShapeDtypeStruct((groups, lanes), f32),
        ]
        + [jax.ShapeDtypeStruct((users // parts, width), f32)] * parts,
        scratch_shapes=[
            pltpu.VMEM((2 * width, items), bf16),
            pltpu.VMEM((width, items), bf16),
            pltpu.VMEM((items, 2 * width), bf16),
            pltpu.VMEM((users, items), jnp.int32),
            pltpu.VMEM((1, items), f32),
            pltpu.VMEM((users, items), bf16),
            pltpu.VMEM((parts, steps, piece, width), f32),
            pltpu.VMEM((parts, users // parts, width), f32),
            pltpu.SemaphoreType.DMA((steps,)),
            pltpu.SemaphoreType.DMA((steps,)),
            pltpu.SemaphoreType.DMA,
        ],
        compiler_params=pltpu.CompilerParams(vmem_limit_bytes=20 << 20),
        cost_estimate=cost(12 * users * items * width),
        name="block",
    )(*user_rows, item_rows, *(pltpu.with_memory_space_constraint(value, pltpu.HBM) for value in (prefs, rate)))


def relay_kernel(own_ref, one_ref, two_ref, three_ref, *more_refs):
    *out_refs, sum_ref = more_refs
    piece = out_refs[0].shape[0]
    sum_ref[...] = own_ref[...] + one_ref[...] + two_ref[...] + three_ref[...]
    mine = lax.axis_index("run")
    for shift, out_ref in enumerate(out_refs):
        start = pl.multiple_of(lax.rem(mine + shift, len(out_refs)) * piece, piece)
        out_ref[...] = sum_ref[pl.ds(start, piece), :]


def relay(parts):
    rows, width = parts[0].shape
    count = len(parts)
    return pl.pallas_call(
        relay_kernel,
        in_specs=[whole] * count,
        out_specs=[whole] * count,
        out_shape=[jax.ShapeDtypeStruct((rows // count, width), f32)] * count,
        scratch_shapes=[pltpu.VMEM((rows, width), f32)],
        compiler_params=pltpu.CompilerParams(vmem_limit_bytes=8 << 20),
        cost_estimate=cost(1 << 20),
        name="relay",
    )(*parts)


def item_kernel(bound_scale, all_sq_ref, norm_ref, clip_ref, turned_ref, high_ref, far_ref, keep_ref, give_ref, pair_ref, low_ref, first_ref, ready):
    width, users = turned_ref.shape
    items = high_ref.shape[1]
    bit = keep_ref.shape[1]
    tile = 2 * lanes
    first = lax.axis_index("core") == 0
    spans = [slice(part * tile, (part + 1) * tile) for part in range(users // tile)]
    copies = [pltpu.make_async_copy(far_ref.at[span], low_ref.at[span], ready.at[part]) for part, span in enumerate(spans)]
    for copy in copies:
        copy.start()
    total = jnp.sum(all_sq_ref[...], axis=0)
    bound = clip_ref[...].astype(f32) * bound_scale
    factor = jnp.minimum(1.0, bound / jnp.sqrt(total * norm_ref[...] + 1e-06))
    for part in range(users // lanes):
        place = slice(part * lanes, (part + 1) * lanes)
        pair_ref[:width, place], pair_ref[width:, place] = halves(turned_ref[:, place] * factor[part : part + 1, :])
    for part in range(items // tile):
        place = slice(part * tile, (part + 1) * tile)
        tall = product(pair_ref[...], high_ref[:, place])
        first_ref[:, place] = tall[:width] + tall[width:]
    for copy in copies:
        copy.wait()
    for part in range(items // tile):
        place = slice(part * tile, (part + 1) * tile)
        summed = first_ref[:, place] + product(pair_ref[:width, :], low_ref[:, place])
        for inner in range(tile // lanes):
            rows = summed[:, inner * lanes : (inner + 1) * lanes].T
            for piece in range(lanes // (2 * bit)):
                index = (part * tile + inner * lanes) // (2 * bit) + piece
                even = rows[2 * piece * bit : (2 * piece + 1) * bit, :]
                odd = rows[(2 * piece + 1) * bit : (2 * piece + 2) * bit, :]
                keep_ref[index] = jnp.where(first, even, odd)
                give_ref[index] = jnp.where(first, odd, even)


def item_gradients(bound_scale, all_sq, norm, clip, turned, high, low, bit):
    users, items = high.shape
    width = turned.shape[0]

    def body(*refs):
        item_kernel(bound_scale, *refs)

    return pl.pallas_call(
        body,
        in_specs=[whole] * 5 + [far],
        out_specs=[whole] * 2,
        out_shape=[jax.ShapeDtypeStruct((items // (2 * bit), bit, width), f32)] * 2,
        scratch_shapes=[
            pltpu.VMEM((2 * width, users), bf16),
            pltpu.VMEM((users, items), bf16),
            pltpu.VMEM((width, items), f32),
            pltpu.SemaphoreType.DMA((users // (2 * lanes),)),
        ],
        compiler_params=pltpu.CompilerParams(vmem_limit_bytes=12 << 20),
        cost_estimate=cost(6 * users * items * width),
        name="item_gradients",
    )(all_sq, norm, clip, turned, high, pltpu.with_memory_space_constraint(low, pltpu.HBM))


def join_kernel(keep_ref, both_ref, out_ref):
    out_ref[...] = keep_ref[...] + both_ref[1 - lax.axis_index("core")]


def join(keep, both):
    return pl.pallas_call(
        join_kernel,
        in_specs=[whole] * 2,
        out_specs=whole,
        out_shape=jax.ShapeDtypeStruct(keep.shape, f32),
        compiler_params=pltpu.CompilerParams(vmem_limit_bytes=8 << 20),
        cost_estimate=cost(1 << 20),
        name="join",
    )(keep, both)


def fold_kernel(tiles_ref, keep_ref, give_ref):
    mine = lax.axis_index("half")
    keep_ref[...] = jnp.sum(tiles_ref[:, mine], axis=0)
    give_ref[...] = jnp.sum(tiles_ref[:, 1 - mine], axis=0)


def fold(tiles):
    return pl.pallas_call(
        fold_kernel,
        in_specs=[whole],
        out_specs=[whole] * 2,
        out_shape=[jax.ShapeDtypeStruct(tiles.shape[2:], f32)] * 2,
        compiler_params=pltpu.CompilerParams(vmem_limit_bytes=8 << 20),
        cost_estimate=cost(1 << 20),
        name="fold",
    )(tiles)


def step_of(emb, acc, gradient):
    new_acc = acc + gradient * gradient
    return emb - learn_rate * gradient / jnp.sqrt(new_acc), new_acc


def finish_kernel(
    own_ref, one_ref, two_ref, three_ref, keep_ref, both_ref, user_ref, user_acc_ref, item_ref, item_acc_ref, noise_ref,
    user_out, user_acc_out, item_out, item_acc_out
):
    user_grad = own_ref[...] + one_ref[...] + two_ref[...] + three_ref[...]
    user_out[...], user_acc_out[...] = step_of(user_ref[...], user_acc_ref[...], user_grad)
    item_grad = keep_ref[...] + both_ref[1 - lax.axis_index("half")] + noise_step * noise_ref[...].astype(f32)
    item_out[...], item_acc_out[...] = step_of(item_ref[...], item_acc_ref[...], item_grad)


def finish(parts, keep, both, user_emb, user_acc, item_emb, item_acc, noise):
    user = jax.ShapeDtypeStruct(user_emb.shape, f32)
    item = jax.ShapeDtypeStruct(item_emb.shape, f32)
    return pl.pallas_call(
        finish_kernel,
        in_specs=[whole] * (7 + len(parts)),
        out_specs=[whole] * 4,
        out_shape=[user, user, item, item],
        compiler_params=pltpu.CompilerParams(vmem_limit_bytes=8 << 20),
        name="finish",
    )(*parts, keep, both, user_emb, user_acc, item_emb, item_acc, noise)


def passed_round(parts, axis):
    count = lax.axis_size(axis)
    moved = [
        lax.ppermute(part, axis, [(place, (place + shift) % count) for place in range(count)])
        for shift, part in enumerate(parts)
        if shift
    ]
    return [parts[0], *moved]


def exchange(value, axis):
    return lax.all_to_all(value, axis, 0, 0, tiled=True)


def from_everyone(value, axis):
    return exchange(jnp.broadcast_to(value[None], (lax.axis_size(axis), *value.shape)), axis)


def local(prefs, item_weight, clip_units, user_emb, user_acc, item_emb, item_acc, noise):
    users, items = prefs.shape
    _, width = user_emb.shape
    bit = item_emb.shape[0]
    groups = users // lanes
    bound_scale = 0.001 * (items * lax.axis_size(item_axes) * width) ** 0.5
    user_run = from_everyone(user_emb, "run")
    item_pair = lax.all_gather(item_emb, "half")
    item_line = from_everyone(item_pair, "z").reshape(-1, bit, width)
    user_rows = passed_round([user_run] * lax.axis_size("x"), "x")
    item_rows = lax.all_gather(item_line, "core")
    high, low, sq, turned, norm, *parts = block(user_rows, item_rows, prefs, item_weight.reshape(1, items))
    all_sq = from_everyone(sq, item_axes)
    parts = passed_round(parts, "x")
    parts = relay(parts)
    parts = passed_round(parts, "run")
    keep, give = item_gradients(bound_scale, all_sq, norm, clip_units.reshape(groups, lanes), turned, high, low, bit)
    joined = join(keep, lax.all_gather(give, "core"))
    tiles = exchange(joined.reshape(-1, 2, bit, width), "z")
    keep, give = fold(tiles)
    both = lax.all_gather(give, "half")
    return tuple(finish(parts, keep, both, user_emb, user_acc, item_emb, item_acc, noise))


def solution(mesh):
    fine = Mesh(mesh.devices.reshape(sizes), names)
    by_user = P(user_axes + item_axes, None)
    by_item = P(item_axes + user_axes, None)
    return jax.shard_map(
        local,
        mesh=fine,
        in_specs=(P(user_axes, item_axes), P(item_axes), P(user_axes), by_user, by_user, by_item, by_item, by_item),
        out_specs=(by_user, by_user, by_item, by_item),
        check_vma=False,
    )
```

time: 104 us -> 108 us (1.038)
  the two profiles are of different devices: /device:TPU:8 before, /device:TPU:6 now
where the time goes in v2:
time: 108 us; the launch traced here: 107 us
  starting transfers between devices  51.3 us (48%)
  blocking collectives  36.3 us (34%)
  Pallas kernels  9.57 us (9%)
  waiting for transfers between devices  6.75 us (6%)
  local copies, waits for them, and re-layouts  2.19 us (2%)
    ppermute x9, starting transfers between devices, passed_round(): lax.ppermute(part, axis, [(place, (place + shift) % count) for place in r...  29 us
    all_to_all x3, starting transfers between devices, exchange(): return lax.all_to_all(value, axis, 0, 0, tiled=True)  22.4 us
    all_to_all x1, blocking collectives, exchange(): return lax.all_to_all(value, axis, 0, 0, tiled=True)  15 us
    all_gather x1, blocking collectives, local(): item_pair = lax.all_gather(item_emb, 'half')  8.58 us
    all_gather x1, blocking collectives, local(): both = lax.all_gather(give, 'half')  8.31 us
    ppermute x9, waiting for transfers between devices, passed_round(): lax.ppermute(part, axis, [(place, (place + shift) % count) for place in r...  5.97 us
    pallas_call x1, Pallas kernels, block(): pl.pallas_call(block_kernel, in_specs=[whole] * (parts + 1) + [far] * 2,...  5.71 us
    pallas_call x1, Pallas kernels, item_gradients(): pl.pallas_call(body, in_specs=[whole] * 5 + [far], out_specs=[whole] * 2,...  2.4 us
  transfers between devices with their start and end apart: 12, of which 4 were waited for; matrix products, arithmetic and copies ran while one was open for 0% of the time, Pallas kernels for 0%

profile of v2, /device:TPU:6, one launch (start us, length us, event | category | flops | bytes accessed | tf_op | source)
XLA Modules:
  0.0 107.0 jit_solution(10581189456053662035)
XLA Ops:
  0.6 1.4 %broadcast_in_dim.6 = f32[4,64,128]{2,1,0:T(8,128)} broadcast(f32[64,128]{1,0:T(8,128)} %user_ref.1), dimensions={1,2} | broadcast | bytes 163840 | tf_op jit(solution)/shard_map/broadcast_in_dim | solution.py:303
  2.0 4.9 %all-to-all-start = ((f32[4,64,128]{2,1,0:T(8,128)}), f32[4,64,128]{2,1,0:T(8,128)S(1)}, u32[]{:S(2)}, u32[]{:S(2)}) async-start(f32[4,64,128]{2,1,0:T(8,128)} %broadcast_in_dim.6), calls=%async_computation | async-start | bytes 262144 | tf_op jit(solution)/shard_map/all_to_all | solution.py:299
  6.9 8.6 %all-gather = f32[64,128]{1,0:T(8,128)S(1)} all-gather(f32[32,128]{1,0:T(8,128)} %item_ref.1), channel_id=2, replica_groups=mesh['z'=8,'half'=2,'core'=2,'run'=4,'x'=4] {'half'}, dimensions={0}, use_global_device_ids=true | all-gather | bytes 49152 | tf_op jit(solution)/shard_map/all_gather | solution.py:313
  15.5 0.7 broadcast_in_dim.7
  16.2 10.3 %all-to-all-start.1 = ((f32[8,2,32,128]{3,2,1,0:T(8,128)}), f32[8,2,32,128]{3,2,1,0:T(8,128)S(1)}, u32[]{:S(2)}, u32[]{:S(2)}) async-start(f32[8,2,32,128]{3,2,1,0:T(8,128)} %broadcast_in_dim.7), calls=%async_computation.1 | async-start | bytes 524288 | tf_op jit(solution)/shard_map/all_to_all | solution.py:299
  26.6 2.7 %collective-permute-start.2 = (f32[4,64,128]{2,1,0:T(8,128)S(1)}, f32[4,64,128]{2,1,0:T(8,128)S(1)}, u32[]{:S(2)}, u32[]{:S(2)}) collective-permute-start(f32[4,64,128]{2,1,0:T(8,128)S(1)} %all-to-all-done.own_ref), channel_id=1, source_target_pairs={{0,3},{1,0},{2,1},{3,2},{4,7},{5,4},{6,5},{7,6},{8,11},{9,8},{10,9... | collective-permute-start | bytes 393224 | tf_op jit(solution)/shard_map/ppermute | solution.py:291
  29.3 3.0 %collective-permute-start.1 = (f32[4,64,128]{2,1,0:T(8,128)S(1)}, f32[4,64,128]{2,1,0:T(8,128)S(1)}, u32[]{:S(2)}, u32[]{:S(2)}) collective-permute-start(f32[4,64,128]{2,1,0:T(8,128)S(1)} %all-to-all-done.own_ref), channel_id=1, source_target_pairs={{0,2},{1,3},{2,0},{3,1},{4,6},{5,7},{6,4},{7,5},{8,10},{9,11},{10,... | collective-permute-start | bytes 393224 | tf_op jit(solution)/shard_map/ppermute | solution.py:291
  32.3 4.0 %collective-permute-start = (f32[4,64,128]{2,1,0:T(8,128)S(1)}, f32[4,64,128]{2,1,0:T(8,128)S(1)}, u32[]{:S(2)}, u32[]{:S(2)}) collective-permute-start(f32[4,64,128]{2,1,0:T(8,128)S(1)} %all-to-all-done.own_ref), channel_id=1, source_target_pairs={{0,1},{1,2},{2,3},{3,0},{4,5},{5,6},{6,7},{7,4},{8,9},{9,10},{10,1... | collective-permute-start | bytes 393224 | tf_op jit(solution)/shard_map/ppermute | solution.py:291
  36.3 0.8 all-to-all-done.1
  37.1 2.2 %all_gather.23.item_ref = f32[2,16,32,128]{3,2,1,0:T(8,128)S(1)} all-gather(f32[1,16,32,128]{3,2,1,0:T(8,128)S(1)} %bitcast.10), channel_id=1, replica_groups=mesh['z'=8,'half'=2,'core'=2,'run'=4,'x'=4] {'core'}, dimensions={0}, use_global_device_ids=true | all-gather | bytes 786432 | tf_op jit(solution)/shard_map/all_gather | solution.py:316
  39.3 0.0 collective-permute-done.one_ref
  39.3 5.7 %block.1 = (bf16[1024,1024]{1,0:T(8,128)(2,1)S(1)}, bf16[1024,1024]{1,0:T(8,128)(2,1)}, f32[8,128]{1,0:T(8,128)S(1)}, f32[128,1024]{1,0:T(8,128)S(1)}, f32[8,128...) custom-call(f32[4,64,128]{2,1,0:T(8,128)S(1)} %all-to-all-done.own_r, ...), custom_call_target="tpu_custom_call" | custom-call | flops 1610612736 | bytes 1048576 | tf_op jit(solution)/shard_map/block/pallas_call | solution.py:111
  45.0 15.0 %all_to_all.20.refs_0_ = f32[16,8,128]{2,1,0:T(8,128)S(1)} all-to-all(f32[16,8,128]{2,1,0:T(8,128)S(1)} %broadcast_in_dim.8), channel_id=1, replica_groups=mesh['z'=8,'half'=2,'core'=2,'run'=4,'x'=4] {'run','x'}, dimensions={0} | all-to-all | bytes 131072 | tf_op jit(solution)/shard_map/all_to_all | solution.py:299
  60.0 2.4 %item_gradients.1 = (f32[16,32,128]{2,1,0:T(8,128)S(1)}, f32[16,32,128]{2,1,0:T(8,128)S(1)}) custom-call(f32[16,8,128]{2,1,0:T(8,128)S(1)} %all_to_all.20.refs_0_, f32[8,128]{1,0:T(8,128)S(1)} %get-tuple-element.30.refs_1_, s32[8,128]{1,0:T(8,128)S(1)} %bitcast.9, f32[128,1024]{1,0:T(8,128)S(1)} %get-tuple-element.31.refs_3_, ...), custom_call_target="tpu_custom_call" | custom-call | flops 805306368 | bytes 1048576 | tf_op jit(solution)/shard_map/item_gradients/pallas_call | solution.py:209
  62.4 0.0 copy-start
  62.4 0.0 copy-start.1
  62.4 0.0 copy-start.2
  62.5 0.0 copy-start.4
  62.5 2.3 %all-gather.1 = f32[32,32,128]{2,1,0:T(8,128)S(1)} all-gather(f32[16,32,128]{2,1,0:T(8,128)S(1)} %get-tuple-element.35), channel_id=3, replica_groups=mesh['z'=8,'half'=2,'core'=2,'run'=4,'x'=4] {'core'}, dimensions={0}, use_global_device_ids=true | all-gather | bytes 786432 | tf_op jit(solution)/shard_map/all_gather | solution.py:323
  64.8 0.7 join.1
  65.5 7.2 %all-to-all-start.3 = ((f32[8,2,32,128]{3,2,1,0:T(8,128)}), f32[8,2,32,128]{3,2,1,0:T(8,128)S(1)}, u32[]{:S(2)}, u32[]{:S(2)}) async-start(f32[8,2,32,128]{3,2,1,0:T(8,128)} %bitcast.5), calls=%async_computation.3 | async-start | bytes 524288 | tf_op jit(solution)/shard_map/all_to_all | solution.py:299
  72.7 4.4 %collective-permute-start.3 = (f32[256,128]{1,0:T(8,128)S(1)}, f32[256,128]{1,0:T(8,128)S(1)}, u32[]{:S(2)}, u32[]{:S(2)}) collective-permute-start(f32[256,128]{1,0:T(8,128)S(1)} %get-tuple-element.22), channel_id=1, source_target_pairs={{0,1},{1,2},{2,3},{3,0},{4,5},{5,6},{6,7},{7,4},{8,9},{9,10},{10,1... | collective-permute-start | bytes 393224 | tf_op jit(solution)/shard_map/ppermute | solution.py:291
  77.1 2.3 %collective-permute-start.4 = (f32[256,128]{1,0:T(8,128)S(1)}, f32[256,128]{1,0:T(8,128)S(1)}, u32[]{:S(2)}, u32[]{:S(2)}) collective-permute-start(f32[256,128]{1,0:T(8,128)S(1)} %get-tuple-element.23), channel_id=1, source_target_pairs={{0,2},{1,3},{2,0},{3,1},{4,6},{5,7},{6,4},{7,5},{8,10},{9,11},{10,... | collective-permute-start | bytes 393224 | tf_op jit(solution)/shard_map/ppermute | solution.py:291
  79.4 3.0 %collective-permute-start.5 = (f32[256,128]{1,0:T(8,128)S(1)}, f32[256,128]{1,0:T(8,128)S(1)}, u32[]{:S(2)}, u32[]{:S(2)}) collective-permute-start(f32[256,128]{1,0:T(8,128)S(1)} %get-tuple-element.24), channel_id=1, source_target_pairs={{0,3},{1,0},{2,1},{3,2},{4,7},{5,4},{6,5},{7,6},{8,11},{9,8},{10,9... | collective-permute-start | bytes 393224 | tf_op jit(solution)/shard_map/ppermute | solution.py:291
  82.4 0.3 collective-permute-done.3.one_ref
  82.7 3.7 %collective-permute-done.4.two_ref = f32[256,128]{1,0:T(8,128)S(1)} collective-permute-done((f32[256,128]{1,0:T(8,128)S(1)}, f32[256,128]{1,0:T(8,128)S(1)}, u32[]{:S(2)}, u32[]{:S(2)}) %collective-permute-start.4) | collective-permute-done | bytes 131104 | tf_op jit(solution)/shard_map/ppermute | solution.py:291
  86.4 1.9 %collective-permute-done.5.three_ref = f32[256,128]{1,0:T(8,128)S(1)} collective-permute-done((f32[256,128]{1,0:T(8,128)S(1)}, f32[256,128]{1,0:T(8,128)S(1)}, u32[]{:S(2)}, u32[]{:S(2)}) %collective-permute-start.5) | collective-permute-done | bytes 131104 | tf_op jit(solution)/shard_map/ppermute | solution.py:291
  88.4 2.1 %collective-permute-start.6 = (f32[64,128]{1,0:T(8,128)S(1)}, f32[64,128]{1,0:T(8,128)S(1)}, u32[]{:S(2)}, u32[]{:S(2)}) collective-permute-start(f32[64,128]{1,0:T(8,128)S(1)} %get-tuple-element.26), channel_id=1, source_target_pairs={{0,4},{4,8},{8,12},{12,0},{1,5},{5,9},{9,13},{13,1},{2,6},{6,10},{... | collective-permute-start | bytes 98312 | tf_op jit(solution)/shard_map/ppermute | solution.py:291
  90.4 2.7 %collective-permute-start.7 = (f32[64,128]{1,0:T(8,128)S(1)}, f32[64,128]{1,0:T(8,128)S(1)}, u32[]{:S(2)}, u32[]{:S(2)}) collective-permute-start(f32[64,128]{1,0:T(8,128)S(1)} %get-tuple-element.27), channel_id=1, source_target_pairs={{0,8},{4,12},{8,0},{12,4},{1,9},{5,13},{9,1},{13,5},{2,10},{6,14},... | collective-permute-start | bytes 98312 | tf_op jit(solution)/shard_map/ppermute | solution.py:291
  93.2 4.8 %collective-permute-start.8 = (f32[64,128]{1,0:T(8,128)S(1)}, f32[64,128]{1,0:T(8,128)S(1)}, u32[]{:S(2)}, u32[]{:S(2)}) collective-permute-start(f32[64,128]{1,0:T(8,128)S(1)} %get-tuple-element.28), channel_id=1, source_target_pairs={{0,12},{4,0},{8,4},{12,8},{1,13},{5,1},{9,5},{13,9},{2,14},{6,2},{... | collective-permute-start | bytes 98312 | tf_op jit(solution)/shard_map/ppermute | solution.py:291
  98.0 8.3 %all-gather.2 = f32[64,128]{1,0:T(8,128)S(1)} all-gather(f32[32,128]{1,0:T(8,128)S(1)} %get-tuple-element.37), channel_id=4, replica_groups=mesh['z'=8,'half'=2,'core'=2,'run'=4,'x'=4] {'half'}, dimensions={0}, use_global_device_ids=true | all-gather | bytes 49152 | tf_op jit(solution)/shard_map/all_gather | solution.py:326
  106.4 0.7 finish.1
  (18 shorter events, 0.1 us)
Async XLA Ops:
  2.0 13.5 %all-to-all-start = ((f32[4,64,128]{2,1,0:T(8,128)}), f32[4,64,128]{2,1,0:T(8,128)S(1)}, u32[]{:S(2)}, u32[]{:S(2)}) async-start(f32[4,64,128]{2,1,0:T(8,128)} %broadcast_in_dim.6), calls=%async_computation | async-start | bytes 262144 | tf_op jit(solution)/shard_map/all_to_all | solution.py:299
  16.2 20.9 %all-to-all-start.1 = ((f32[8,2,32,128]{3,2,1,0:T(8,128)}), f32[8,2,32,128]{3,2,1,0:T(8,128)S(1)}, u32[]{:S(2)}, u32[]{:S(2)}) async-start(f32[8,2,32,128]{3,2,1,0:T(8,128)} %broadcast_in_dim.7), calls=%async_computation.1 | async-start | bytes 524288 | tf_op jit(solution)/shard_map/all_to_all | solution.py:299
  26.6 12.7 %collective-permute-start.2 = (f32[4,64,128]{2,1,0:T(8,128)S(1)}, f32[4,64,128]{2,1,0:T(8,128)S(1)}, u32[]{:S(2)}, u32[]{:S(2)}) collective-permute-start(f32[4,64,128]{2,1,0:T(8,128)S(1)} %all-to-all-done.own_ref), channel_id=1, source_target_pairs={{0,3},{1,0},{2,1},{3,2},{4,7},{5,4},{6,5},{7,6},{8,11},{9,8},{10,9... | collective-permute-start | bytes 393224 | tf_op jit(solution)/shard_map/ppermute | solution.py:291
  29.3 10.0 %collective-permute-start.1 = (f32[4,64,128]{2,1,0:T(8,128)S(1)}, f32[4,64,128]{2,1,0:T(8,128)S(1)}, u32[]{:S(2)}, u32[]{:S(2)}) collective-permute-start(f32[4,64,128]{2,1,0:T(8,128)S(1)} %all-to-all-done.own_ref), channel_id=1, source_target_pairs={{0,2},{1,3},{2,0},{3,1},{4,6},{5,7},{6,4},{7,5},{8,10},{9,11},{10,... | collective-permute-start | bytes 393224 | tf_op jit(solution)/shard_map/ppermute | solution.py:291
  32.3 7.0 %collective-permute-start = (f32[4,64,128]{2,1,0:T(8,128)S(1)}, f32[4,64,128]{2,1,0:T(8,128)S(1)}, u32[]{:S(2)}, u32[]{:S(2)}) collective-permute-start(f32[4,64,128]{2,1,0:T(8,128)S(1)} %all-to-all-done.own_ref), channel_id=1, source_target_pairs={{0,1},{1,2},{2,3},{3,0},{4,5},{5,6},{6,7},{7,4},{8,9},{9,10},{10,1... | collective-permute-start | bytes 393224 | tf_op jit(solution)/shard_map/ppermute | solution.py:291
  39.3 20.7 %copy-start.5 = (s32[1024]{0:T(1024)S(1)}, s32[1024]{0:T(1024)}, u32[]{:S(2)}) copy-start(s32[1024]{0:T(1024)} %param.10) | copy-start | bytes 12292
  62.4 43.9 %copy-start = (f32[64,128]{1,0:T(8,128)S(1)}, f32[64,128]{1,0:T(8,128)}, u32[]{:S(2)}) copy-start(f32[64,128]{1,0:T(8,128)} %user_ref.1) | copy-start | bytes 98308
  62.4 43.9 %copy-start.1 = (f32[32,128]{1,0:T(8,128)S(1)}, f32[32,128]{1,0:T(8,128)}, u32[]{:S(2)}) copy-start(f32[32,128]{1,0:T(8,128)} %item_ref.1) | copy-start | bytes 49156
  62.4 43.9 %copy-start.2 = (f32[64,128]{1,0:T(8,128)S(1)}, f32[64,128]{1,0:T(8,128)}, u32[]{:S(2)}) copy-start(f32[64,128]{1,0:T(8,128)} %user_acc_ref.1) | copy-start | bytes 98308
  62.5 43.9 %copy-start.3 = (f32[32,128]{1,0:T(8,128)S(1)}, f32[32,128]{1,0:T(8,128)}, u32[]{:S(2)}) copy-start(f32[32,128]{1,0:T(8,128)} %item_acc_ref.1) | copy-start | bytes 49156
  62.5 43.9 %copy-start.4 = (s32[32,128]{1,0:T(8,128)S(1)}, s32[32,128]{1,0:T(8,128)}, u32[]{:S(2)}) copy-start(s32[32,128]{1,0:T(8,128)} %noise_ref.1) | copy-start | bytes 49156
  65.5 32.4 %all-to-all-start.3 = ((f32[8,2,32,128]{3,2,1,0:T(8,128)}), f32[8,2,32,128]{3,2,1,0:T(8,128)S(1)}, u32[]{:S(2)}, u32[]{:S(2)}) async-start(f32[8,2,32,128]{3,2,1,0:T(8,128)} %bitcast.5), calls=%async_computation.3 | async-start | bytes 524288 | tf_op jit(solution)/shard_map/all_to_all | solution.py:299
  72.7 10.0 %collective-permute-start.3 = (f32[256,128]{1,0:T(8,128)S(1)}, f32[256,128]{1,0:T(8,128)S(1)}, u32[]{:S(2)}, u32[]{:S(2)}) collective-permute-start(f32[256,128]{1,0:T(8,128)S(1)} %get-tuple-element.22), channel_id=1, source_target_pairs={{0,1},{1,2},{2,3},{3,0},{4,5},{5,6},{6,7},{7,4},{8,9},{9,10},{10,1... | collective-permute-start | bytes 393224 | tf_op jit(solution)/shard_map/ppermute | solution.py:291
  77.1 9.3 %collective-permute-start.4 = (f32[256,128]{1,0:T(8,128)S(1)}, f32[256,128]{1,0:T(8,128)S(1)}, u32[]{:S(2)}, u32[]{:S(2)}) collective-permute-start(f32[256,128]{1,0:T(8,128)S(1)} %get-tuple-element.23), channel_id=1, source_target_pairs={{0,2},{1,3},{2,0},{3,1},{4,6},{5,7},{6,4},{7,5},{8,10},{9,11},{10,... | collective-permute-start | bytes 393224 | tf_op jit(solution)/shard_map/ppermute | solution.py:291
  79.4 8.9 %collective-permute-start.5 = (f32[256,128]{1,0:T(8,128)S(1)}, f32[256,128]{1,0:T(8,128)S(1)}, u32[]{:S(2)}, u32[]{:S(2)}) collective-permute-start(f32[256,128]{1,0:T(8,128)S(1)} %get-tuple-element.24), channel_id=1, source_target_pairs={{0,3},{1,0},{2,1},{3,2},{4,7},{5,4},{6,5},{7,6},{8,11},{9,8},{10,9... | collective-permute-start | bytes 393224 | tf_op jit(solution)/shard_map/ppermute | solution.py:291
  88.4 17.9 %collective-permute-start.6 = (f32[64,128]{1,0:T(8,128)S(1)}, f32[64,128]{1,0:T(8,128)S(1)}, u32[]{:S(2)}, u32[]{:S(2)}) collective-permute-start(f32[64,128]{1,0:T(8,128)S(1)} %get-tuple-element.26), channel_id=1, source_target_pairs={{0,4},{4,8},{8,12},{12,0},{1,5},{5,9},{9,13},{13,1},{2,6},{6,10},{... | collective-permute-start | bytes 98312 | tf_op jit(solution)/shard_map/ppermute | solution.py:291
  90.4 15.9 %collective-permute-start.7 = (f32[64,128]{1,0:T(8,128)S(1)}, f32[64,128]{1,0:T(8,128)S(1)}, u32[]{:S(2)}, u32[]{:S(2)}) collective-permute-start(f32[64,128]{1,0:T(8,128)S(1)} %get-tuple-element.27), channel_id=1, source_target_pairs={{0,8},{4,12},{8,0},{12,4},{1,9},{5,13},{9,1},{13,5},{2,10},{6,14},... | collective-permute-start | bytes 98312 | tf_op jit(solution)/shard_map/ppermute | solution.py:291
  93.2 13.2 %collective-permute-start.8 = (f32[64,128]{1,0:T(8,128)S(1)}, f32[64,128]{1,0:T(8,128)S(1)}, u32[]{:S(2)}, u32[]{:S(2)}) collective-permute-start(f32[64,128]{1,0:T(8,128)S(1)} %get-tuple-element.28), channel_id=1, source_target_pairs={{0,12},{4,0},{8,4},{12,8},{1,13},{5,1},{9,5},{13,9},{2,14},{6,2},{... | collective-permute-start | bytes 98312 | tf_op jit(solution)/shard_map/ppermute | solution.py:291

commit v3 on v2

--- a/solution.py
+++ b/solution.py
@@ -34,9 +34,9 @@
 
 
 def block_kernel(
-    own_ref, one_ref, two_ref, three_ref, item_ref, far_ref, far_rate_ref, high_ref, low_ref, sq_ref, turned_ref, norm_ref, *more_refs
+    own_ref, one_ref, two_ref, three_ref, item_ref, far_ref, far_rate_ref, high_ref, low_ref, all_sq_ref, turned_ref, norm_ref, *more_refs
 ):
-    *out_refs, pair_ref, rest_ref, tall_ref, prefs_ref, rate_ref, near_ref, user_ref, sum_ref, ready, gone, rated = more_refs
+    *out_refs, pair_ref, rest_ref, tall_ref, prefs_ref, rate_ref, near_ref, user_ref, sum_ref, copies_ref, ready, gone, rated, spread, sent = more_refs
     parts, steps, piece, width = user_ref.shape
     mine = lax.axis_index("x")
     _, items = prefs_ref.shape
@@ -85,41 +85,49 @@
         for part in range(rows // lanes):
             row = step * (rows // lanes) + part
             total = squares[part * lanes : (part + 1) * lanes, :].T
-            sq_ref[row : row + 1, :] = jnp.sum(total, axis=0, keepdims=True)
-    for step, span in enumerate(blocks):
-        user = user_ref[:, step].reshape(rows, width)
+            sums = jnp.sum(total, axis=0, keepdims=True)
+            for peer in range(copies_ref.shape[0]):
+                copies_ref[peer, row : row + 1, :] = sums
         wide = product(high_ref[span, :], tall_ref[...])
         gradient = wide[:, :width] + wide[:, width:] + product(near_ref[span, :], tall_ref[:, :width])
         for part in range(parts):
             sum_ref[part, step * piece : (step + 1) * piece, :] = gradient[part * piece : (part + 1) * piece, :]
+    stores.append(pltpu.make_async_copy(copies_ref, all_sq_ref, spread))
+    for shift in range(1, parts):
+        stores.append(pltpu.make_async_copy(sum_ref.at[lax.rem(mine + shift, parts)], out_refs[shift], sent.at[shift - 1]))
+    for store in stores[steps:]:
+        store.start()
+    out_refs[0][...] = sum_ref[mine]
+    for step in range(steps):
+        user = user_ref[:, step].reshape(rows, width)
         for part in range(rows // lanes):
             row = step * (rows // lanes) + part
             turned = user[part * lanes : (part + 1) * lanes, :].T
             turned_ref[:, row * lanes : (row + 1) * lanes] = turned
             norm_ref[row : row + 1, :] = jnp.sum(turned * turned, axis=0, keepdims=True)
-    for shift, out_ref in enumerate(out_refs):
-        out_ref[...] = sum_ref[lax.rem(mine + shift, parts)]
     for store in stores:
         store.wait()
 
 
 def block(user_rows, item_rows, prefs, rate):
     parts = len(user_rows)
+    peers = lax.axis_size(item_axes)
     steps, piece, width = user_rows[0].shape
     users, items = prefs.shape
     groups = users // lanes
     return pl.pallas_call(
         block_kernel,
         in_specs=[whole] * (parts + 1) + [far] * 2,
-        out_specs=[whole, far] + [whole] * (3 + parts),
+        out_specs=[whole, far, far] + [whole] * 3 + [far] * (parts - 1),
         out_shape=[
             jax.ShapeDtypeStruct((users, items), bf16),
             pltpu.HBM((users, items), bf16),
-            jax.ShapeDtypeStruct((groups, lanes), f32),
+            pltpu.HBM((peers, groups, lanes), f32),
             jax.ShapeDtypeStruct((width, users), f32),
             jax.ShapeDtypeStruct((groups, lanes), f32),
         ]
-        + [jax.ShapeDtypeStruct((users // parts, width), f32)] * parts,
+        + [jax.ShapeDtypeStruct((users // parts, width), f32)]
+        + [pltpu.HBM((users // parts, width), f32)] * (parts - 1),
         scratch_shapes=[
             pltpu.VMEM((2 * width, items), bf16),
             pltpu.VMEM((width, items), bf16),
@@ -129,9 +137,12 @@
             pltpu.VMEM((users, items), bf16),
             pltpu.VMEM((parts, steps, piece, width), f32),
             pltpu.VMEM((parts, users // parts, width), f32),
+            pltpu.VMEM((peers, groups, lanes), f32),
             pltpu.SemaphoreType.DMA((steps,)),
             pltpu.SemaphoreType.DMA((steps,)),
             pltpu.SemaphoreType.DMA,
+            pltpu.SemaphoreType.DMA,
+            pltpu.SemaphoreType.DMA((parts - 1,)),
         ],
         compiler_params=pltpu.CompilerParams(vmem_limit_bytes=20 << 20),
         cost_estimate=cost(12 * users * items * width),
@@ -184,11 +195,16 @@
         place = slice(part * tile, (part + 1) * tile)
         tall = product(pair_ref[...], high_ref[:, place])
         first_ref[:, place] = tall[:width] + tall[width:]
-    for copy in copies:
+    for span, copy in zip(spans[:-1], copies[:-1]):
         copy.wait()
+        for part in range(items // tile):
+            place = slice(part * tile, (part + 1) * tile)
+            first_ref[:, place] += product(pair_ref[:width, span], low_ref[span, place])
+    last = spans[-1]
+    copies[-1].wait()
     for part in range(items // tile):
         place = slice(part * tile, (part + 1) * tile)
-        summed = first_ref[:, place] + product(pair_ref[:width, :], low_ref[:, place])
+        summed = first_ref[:, place] + product(pair_ref[:width, last], low_ref[last, place])
         for inner in range(tile // lanes):
             rows = summed[:, inner * lanes : (inner + 1) * lanes].T
             for piece in range(lanes // (2 * bit)):
@@ -315,7 +331,7 @@
     user_rows = passed_round([user_run] * lax.axis_size("x"), "x")
     item_rows = lax.all_gather(item_line, "core")
     high, low, sq, turned, norm, *parts = block(user_rows, item_rows, prefs, item_weight.reshape(1, items))
-    all_sq = from_everyone(sq, item_axes)
+    all_sq = exchange(sq, item_axes)
     parts = passed_round(parts, "x")
     parts = relay(parts)
     parts = passed_round(parts, "run")

time: 108 us -> 109 us (level)
  transfers between devices with their start and end apart: 12 -> 12, of which waited for: 4 -> 3; matrix products, arithmetic and copies ran while one was open for 0% -> 0% of each run, Pallas kernels for 0% -> 0%
where the time goes in v3:
time: 109 us; the launch traced here: 108 us
  starting transfers between devices  51.4 us (47%)
  blocking collectives  36.5 us (33%)
  Pallas kernels  9.97 us (9%)
  waiting for transfers between devices  6.72 us (6%)
  local copies, waits for them, and re-layouts  2.19 us (2%)
    ppermute x9, starting transfers between devices, passed_round(): lax.ppermute(part, axis, [(place, (place + shift) % count) for place in r...  29 us
    all_to_all x3, starting transfers between devices, exchange(): return lax.all_to_all(value, axis, 0, 0, tiled=True)  22.4 us
    all_to_all x1, blocking collectives, exchange(): return lax.all_to_all(value, axis, 0, 0, tiled=True)  15.2 us
    all_gather x1, blocking collectives, local(): item_pair = lax.all_gather(item_emb, 'half')  8.58 us
    all_gather x1, blocking collectives, local(): both = lax.all_gather(give, 'half')  8.31 us
    pallas_call x1, Pallas kernels, block(): pl.pallas_call(block_kernel, in_specs=[whole] * (parts + 1) + [far] * 2,...  6.31 us
    ppermute x9, waiting for transfers between devices, passed_round(): lax.ppermute(part, axis, [(place, (place + shift) % count) for place in r...  5.93 us
    all_gather x1, blocking collectives, local(): joined = join(keep, lax.all_gather(give, 'core'))  2.31 us
  transfers between devices with their start and end apart: 12, of which 3 were waited for; matrix products, arithmetic and copies ran while one was open for 0% of the time, Pallas kernels for 0%

profile of v3, /device:TPU:6, one launch (start us, length us, event | category | flops | bytes accessed | tf_op | source)
XLA Modules:
  0.0 107.7 jit_solution(13621574271099763235)
XLA Ops:
  0.6 1.4 %broadcast_in_dim.4 = f32[4,64,128]{2,1,0:T(8,128)} broadcast(f32[64,128]{1,0:T(8,128)} %user_ref.1), dimensions={1,2} | broadcast | bytes 163840 | tf_op jit(solution)/shard_map/broadcast_in_dim | solution.py:319
  2.0 4.9 %all-to-all-start = ((f32[4,64,128]{2,1,0:T(8,128)}), f32[4,64,128]{2,1,0:T(8,128)S(1)}, u32[]{:S(2)}, u32[]{:S(2)}) async-start(f32[4,64,128]{2,1,0:T(8,128)} %broadcast_in_dim.4), calls=%async_computation | async-start | bytes 262144 | tf_op jit(solution)/shard_map/all_to_all | solution.py:315
  6.9 8.6 %all-gather = f32[64,128]{1,0:T(8,128)S(1)} all-gather(f32[32,128]{1,0:T(8,128)} %item_ref.1), channel_id=2, replica_groups=mesh['z'=8,'half'=2,'core'=2,'run'=4,'x'=4] {'half'}, dimensions={0}, use_global_device_ids=true | all-gather | bytes 49152 | tf_op jit(solution)/shard_map/all_gather | solution.py:329
  15.5 0.7 broadcast_in_dim.5
  16.2 10.3 %all-to-all-start.1 = ((f32[8,2,32,128]{3,2,1,0:T(8,128)}), f32[8,2,32,128]{3,2,1,0:T(8,128)S(1)}, u32[]{:S(2)}, u32[]{:S(2)}) async-start(f32[8,2,32,128]{3,2,1,0:T(8,128)} %broadcast_in_dim.5), calls=%async_computation.1 | async-start | bytes 524288 | tf_op jit(solution)/shard_map/all_to_all | solution.py:315
  26.5 2.7 %collective-permute-start.2 = (f32[4,64,128]{2,1,0:T(8,128)S(1)}, f32[4,64,128]{2,1,0:T(8,128)S(1)}, u32[]{:S(2)}, u32[]{:S(2)}) collective-permute-start(f32[4,64,128]{2,1,0:T(8,128)S(1)} %all-to-all-done.own_ref), channel_id=1, source_target_pairs={{0,3},{1,0},{2,1},{3,2},{4,7},{5,4},{6,5},{7,6},{8,11},{9,8},{10,9... | collective-permute-start | bytes 393224 | tf_op jit(solution)/shard_map/ppermute | solution.py:307
  29.3 3.0 %collective-permute-start.1 = (f32[4,64,128]{2,1,0:T(8,128)S(1)}, f32[4,64,128]{2,1,0:T(8,128)S(1)}, u32[]{:S(2)}, u32[]{:S(2)}) collective-permute-start(f32[4,64,128]{2,1,0:T(8,128)S(1)} %all-to-all-done.own_ref), channel_id=1, source_target_pairs={{0,2},{1,3},{2,0},{3,1},{4,6},{5,7},{6,4},{7,5},{8,10},{9,11},{10,... | collective-permute-start | bytes 393224 | tf_op jit(solution)/shard_map/ppermute | solution.py:307
  32.3 4.0 %collective-permute-start = (f32[4,64,128]{2,1,0:T(8,128)S(1)}, f32[4,64,128]{2,1,0:T(8,128)S(1)}, u32[]{:S(2)}, u32[]{:S(2)}) collective-permute-start(f32[4,64,128]{2,1,0:T(8,128)S(1)} %all-to-all-done.own_ref), channel_id=1, source_target_pairs={{0,1},{1,2},{2,3},{3,0},{4,5},{5,6},{6,7},{7,4},{8,9},{9,10},{10,1... | collective-permute-start | bytes 393224 | tf_op jit(solution)/shard_map/ppermute | solution.py:307
  36.3 0.8 all-to-all-done.1
  37.1 2.2 %all_gather.23.item_ref = f32[2,16,32,128]{3,2,1,0:T(8,128)S(1)} all-gather(f32[1,16,32,128]{3,2,1,0:T(8,128)S(1)} %bitcast.10), channel_id=1, replica_groups=mesh['z'=8,'half'=2,'core'=2,'run'=4,'x'=4] {'core'}, dimensions={0}, use_global_device_ids=true | all-gather | bytes 786432 | tf_op jit(solution)/shard_map/all_gather | solution.py:332
  39.3 0.0 collective-permute-done.one_ref
  39.3 6.3 %block.1 = (bf16[1024,1024]{1,0:T(8,128)(2,1)S(1)}, bf16[1024,1024]{1,0:T(8,128)(2,1)}, f32[16,8,128]{2,1,0:T(8,128)}, f32[128,1024]{1,0:T(8,128)S(1)}, f32[8,12...) custom-call(f32[4,64,128]{2,1,0:T(8,128)S(1)} %all-to-all-done.own_r, ...), custom_call_target="tpu_custom_call" | custom-call | flops 1610612736 | bytes 1048576 | tf_op jit(solution)/shard_map/block/pallas_call | solution.py:118
  45.6 15.2 %all_to_all.20.refs_0_ = f32[16,8,128]{2,1,0:T(8,128)S(1)} all-to-all(f32[16,8,128]{2,1,0:T(8,128)} %get-tuple-element.29), channel_id=1, replica_groups=mesh['z'=8,'half'=2,'core'=2,'run'=4,'x'=4] {'run','x'}, dimensions={0} | all-to-all | bytes 131072 | tf_op jit(solution)/shard_map/all_to_all | solution.py:315
  60.8 2.2 %item_gradients.1 = (f32[16,32,128]{2,1,0:T(8,128)S(1)}, f32[16,32,128]{2,1,0:T(8,128)S(1)}) custom-call(f32[16,8,128]{2,1,0:T(8,128)S(1)} %all_to_all.20.refs_0_, f32[8,128]{1,0:T(8,128)S(1)} %get-tuple-element.30.refs_1_, s32[8,128]{1,0:T(8,128)S(1)} %bitcast.9, f32[128,1024]{1,0:T(8,128)S(1)} %get-tuple-element.31.refs_3_, ...), custom_call_target="tpu_custom_call" | custom-call | flops 805306368 | bytes 1048576 | tf_op jit(solution)/shard_map/item_gradients/pallas_call | solution.py:225
  63.0 0.0 copy-start
  63.1 0.0 copy-start.1
  63.1 0.0 copy-start.2
  63.1 0.0 copy-start.3
  63.1 0.0 copy-start.4
  63.1 2.3 %all-gather.1 = f32[32,32,128]{2,1,0:T(8,128)S(1)} all-gather(f32[16,32,128]{2,1,0:T(8,128)S(1)} %get-tuple-element.35), channel_id=3, replica_groups=mesh['z'=8,'half'=2,'core'=2,'run'=4,'x'=4] {'core'}, dimensions={0}, use_global_device_ids=true | all-gather | bytes 786432 | tf_op jit(solution)/shard_map/all_gather | solution.py:339
  65.4 0.7 join.1
  66.1 7.2 %all-to-all-start.3 = ((f32[8,2,32,128]{3,2,1,0:T(8,128)}), f32[8,2,32,128]{3,2,1,0:T(8,128)S(1)}, u32[]{:S(2)}, u32[]{:S(2)}) async-start(f32[8,2,32,128]{3,2,1,0:T(8,128)} %bitcast.5), calls=%async_computation.3 | async-start | bytes 524288 | tf_op jit(solution)/shard_map/all_to_all | solution.py:315
  73.3 4.4 %collective-permute-start.3 = (f32[256,128]{1,0:T(8,128)S(1)}, f32[256,128]{1,0:T(8,128)S(1)}, u32[]{:S(2)}, u32[]{:S(2)}) collective-permute-start(f32[256,128]{1,0:T(8,128)S(1)} %copy-done.8), channel_id=1, source_target_pairs={{0,1},{1,2},{2,3},{3,0},{4,5},{5,6},{6,7},{7,4},{8,9},{9,10},{10,1... | collective-permute-start | bytes 393224 | tf_op jit(solution)/shard_map/ppermute | solution.py:307
  77.8 2.3 %collective-permute-start.4 = (f32[256,128]{1,0:T(8,128)S(1)}, f32[256,128]{1,0:T(8,128)S(1)}, u32[]{:S(2)}, u32[]{:S(2)}) collective-permute-start(f32[256,128]{1,0:T(8,128)S(1)} %copy-done.7), channel_id=1, source_target_pairs={{0,2},{1,3},{2,0},{3,1},{4,6},{5,7},{6,4},{7,5},{8,10},{9,11},{10,... | collective-permute-start | bytes 393224 | tf_op jit(solution)/shard_map/ppermute | solution.py:307
  80.1 3.0 %collective-permute-start.5 = (f32[256,128]{1,0:T(8,128)S(1)}, f32[256,128]{1,0:T(8,128)S(1)}, u32[]{:S(2)}, u32[]{:S(2)}) collective-permute-start(f32[256,128]{1,0:T(8,128)S(1)} %copy-done.6), channel_id=1, source_target_pairs={{0,3},{1,0},{2,1},{3,2},{4,7},{5,4},{6,5},{7,6},{8,11},{9,8},{10,9... | collective-permute-start | bytes 393224 | tf_op jit(solution)/shard_map/ppermute | solution.py:307
  83.1 3.9 %collective-permute-done.4.two_ref = f32[256,128]{1,0:T(8,128)S(1)} collective-permute-done((f32[256,128]{1,0:T(8,128)S(1)}, f32[256,128]{1,0:T(8,128)S(1)}, u32[]{:S(2)}, u32[]{:S(2)}) %collective-permute-start.4) | collective-permute-done | bytes 131104 | tf_op jit(solution)/shard_map/ppermute | solution.py:307
  87.0 1.9 %collective-permute-done.5.three_ref = f32[256,128]{1,0:T(8,128)S(1)} collective-permute-done((f32[256,128]{1,0:T(8,128)S(1)}, f32[256,128]{1,0:T(8,128)S(1)}, u32[]{:S(2)}, u32[]{:S(2)}) %collective-permute-start.5) | collective-permute-done | bytes 131104 | tf_op jit(solution)/shard_map/ppermute | solution.py:307
  89.0 2.1 %collective-permute-start.6 = (f32[64,128]{1,0:T(8,128)S(1)}, f32[64,128]{1,0:T(8,128)S(1)}, u32[]{:S(2)}, u32[]{:S(2)}) collective-permute-start(f32[64,128]{1,0:T(8,128)S(1)} %get-tuple-element.26), channel_id=1, source_target_pairs={{0,4},{4,8},{8,12},{12,0},{1,5},{5,9},{9,13},{13,1},{2,6},{6,10},{... | collective-permute-start | bytes 98312 | tf_op jit(solution)/shard_map/ppermute | solution.py:307
  91.1 2.7 %collective-permute-start.7 = (f32[64,128]{1,0:T(8,128)S(1)}, f32[64,128]{1,0:T(8,128)S(1)}, u32[]{:S(2)}, u32[]{:S(2)}) collective-permute-start(f32[64,128]{1,0:T(8,128)S(1)} %get-tuple-element.27), channel_id=1, source_target_pairs={{0,8},{4,12},{8,0},{12,4},{1,9},{5,13},{9,1},{13,5},{2,10},{6,14},... | collective-permute-start | bytes 98312 | tf_op jit(solution)/shard_map/ppermute | solution.py:307
  93.8 4.8 %collective-permute-start.8 = (f32[64,128]{1,0:T(8,128)S(1)}, f32[64,128]{1,0:T(8,128)S(1)}, u32[]{:S(2)}, u32[]{:S(2)}) collective-permute-start(f32[64,128]{1,0:T(8,128)S(1)} %get-tuple-element.28), channel_id=1, source_target_pairs={{0,12},{4,0},{8,4},{12,8},{1,13},{5,1},{9,5},{13,9},{2,14},{6,2},{... | collective-permute-start | bytes 98312 | tf_op jit(solution)/shard_map/ppermute | solution.py:307
  98.6 8.3 %all-gather.2 = f32[64,128]{1,0:T(8,128)S(1)} all-gather(f32[32,128]{1,0:T(8,128)S(1)} %get-tuple-element.37), channel_id=4, replica_groups=mesh['z'=8,'half'=2,'core'=2,'run'=4,'x'=4] {'half'}, dimensions={0}, use_global_device_ids=true | all-gather | bytes 49152 | tf_op jit(solution)/shard_map/all_gather | solution.py:342
  107.0 0.7 finish.1
  (23 shorter events, 0.1 us)
Async XLA Ops:
  2.0 13.5 %all-to-all-start = ((f32[4,64,128]{2,1,0:T(8,128)}), f32[4,64,128]{2,1,0:T(8,128)S(1)}, u32[]{:S(2)}, u32[]{:S(2)}) async-start(f32[4,64,128]{2,1,0:T(8,128)} %broadcast_in_dim.4), calls=%async_computation | async-start | bytes 262144 | tf_op jit(solution)/shard_map/all_to_all | solution.py:315
  16.2 20.9 %all-to-all-start.1 = ((f32[8,2,32,128]{3,2,1,0:T(8,128)}), f32[8,2,32,128]{3,2,1,0:T(8,128)S(1)}, u32[]{:S(2)}, u32[]{:S(2)}) async-start(f32[8,2,32,128]{3,2,1,0:T(8,128)} %broadcast_in_dim.5), calls=%async_computation.1 | async-start | bytes 524288 | tf_op jit(solution)/shard_map/all_to_all | solution.py:315
  26.5 12.7 %collective-permute-start.2 = (f32[4,64,128]{2,1,0:T(8,128)S(1)}, f32[4,64,128]{2,1,0:T(8,128)S(1)}, u32[]{:S(2)}, u32[]{:S(2)}) collective-permute-start(f32[4,64,128]{2,1,0:T(8,128)S(1)} %all-to-all-done.own_ref), channel_id=1, source_target_pairs={{0,3},{1,0},{2,1},{3,2},{4,7},{5,4},{6,5},{7,6},{8,11},{9,8},{10,9... | collective-permute-start | bytes 393224 | tf_op jit(solution)/shard_map/ppermute | solution.py:307
  29.3 10.0 %collective-permute-start.1 = (f32[4,64,128]{2,1,0:T(8,128)S(1)}, f32[4,64,128]{2,1,0:T(8,128)S(1)}, u32[]{:S(2)}, u32[]{:S(2)}) collective-permute-start(f32[4,64,128]{2,1,0:T(8,128)S(1)} %all-to-all-done.own_ref), channel_id=1, source_target_pairs={{0,2},{1,3},{2,0},{3,1},{4,6},{5,7},{6,4},{7,5},{8,10},{9,11},{10,... | collective-permute-start | bytes 393224 | tf_op jit(solution)/shard_map/ppermute | solution.py:307
  32.3 7.0 %collective-permute-start = (f32[4,64,128]{2,1,0:T(8,128)S(1)}, f32[4,64,128]{2,1,0:T(8,128)S(1)}, u32[]{:S(2)}, u32[]{:S(2)}) collective-permute-start(f32[4,64,128]{2,1,0:T(8,128)S(1)} %all-to-all-done.own_ref), channel_id=1, source_target_pairs={{0,1},{1,2},{2,3},{3,0},{4,5},{5,6},{6,7},{7,4},{8,9},{9,10},{10,1... | collective-permute-start | bytes 393224 | tf_op jit(solution)/shard_map/ppermute | solution.py:307
  39.3 21.5 %copy-start.5 = (s32[1024]{0:T(1024)S(1)}, s32[1024]{0:T(1024)}, u32[]{:S(2)}) copy-start(s32[1024]{0:T(1024)} %param.10) | copy-start | bytes 12292
  63.0 10.3 %copy-start.8 = (f32[256,128]{1,0:T(8,128)S(1)}, f32[256,128]{1,0:T(8,128)}, u32[]{:S(2)}) copy-start(f32[256,128]{1,0:T(8,128)} %get-tuple-element.22) | copy-start | bytes 393220
  63.0 14.7 %copy-start.7 = (f32[256,128]{1,0:T(8,128)S(1)}, f32[256,128]{1,0:T(8,128)}, u32[]{:S(2)}) copy-start(f32[256,128]{1,0:T(8,128)} %get-tuple-element.23) | copy-start | bytes 393220
  63.0 17.0 %copy-start.6 = (f32[256,128]{1,0:T(8,128)S(1)}, f32[256,128]{1,0:T(8,128)}, u32[]{:S(2)}) copy-start(f32[256,128]{1,0:T(8,128)} %get-tuple-element.24) | copy-start | bytes 393220
  63.0 43.9 %copy-start = (f32[64,128]{1,0:T(8,128)S(1)}, f32[64,128]{1,0:T(8,128)}, u32[]{:S(2)}) copy-start(f32[64,128]{1,0:T(8,128)} %user_ref.1) | copy-start | bytes 98308
  63.1 43.9 %copy-start.1 = (f32[32,128]{1,0:T(8,128)S(1)}, f32[32,128]{1,0:T(8,128)}, u32[]{:S(2)}) copy-start(f32[32,128]{1,0:T(8,128)} %item_ref.1) | copy-start | bytes 49156
  63.1 43.9 %copy-start.2 = (f32[64,128]{1,0:T(8,128)S(1)}, f32[64,128]{1,0:T(8,128)}, u32[]{:S(2)}) copy-start(f32[64,128]{1,0:T(8,128)} %user_acc_ref.1) | copy-start | bytes 98308
  63.1 43.9 %copy-start.3 = (f32[32,128]{1,0:T(8,128)S(1)}, f32[32,128]{1,0:T(8,128)}, u32[]{:S(2)}) copy-start(f32[32,128]{1,0:T(8,128)} %item_acc_ref.1) | copy-start | bytes 49156
  63.1 43.9 %copy-start.4 = (s32[32,128]{1,0:T(8,128)S(1)}, s32[32,128]{1,0:T(8,128)}, u32[]{:S(2)}) copy-start(s32[32,128]{1,0:T(8,128)} %noise_ref.1) | copy-start | bytes 49156
  66.1 32.4 %all-to-all-start.3 = ((f32[8,2,32,128]{3,2,1,0:T(8,128)}), f32[8,2,32,128]{3,2,1,0:T(8,128)S(1)}, u32[]{:S(2)}, u32[]{:S(2)}) async-start(f32[8,2,32,128]{3,2,1,0:T(8,128)} %bitcast.5), calls=%async_computation.3 | async-start | bytes 524288 | tf_op jit(solution)/shard_map/all_to_all | solution.py:315
  73.3 9.7 %collective-permute-start.3 = (f32[256,128]{1,0:T(8,128)S(1)}, f32[256,128]{1,0:T(8,128)S(1)}, u32[]{:S(2)}, u32[]{:S(2)}) collective-permute-start(f32[256,128]{1,0:T(8,128)S(1)} %copy-done.8), channel_id=1, source_target_pairs={{0,1},{1,2},{2,3},{3,0},{4,5},{5,6},{6,7},{7,4},{8,9},{9,10},{10,1... | collective-permute-start | bytes 393224 | tf_op jit(solution)/shard_map/ppermute | solution.py:307
  77.8 9.2 %collective-permute-start.4 = (f32[256,128]{1,0:T(8,128)S(1)}, f32[256,128]{1,0:T(8,128)S(1)}, u32[]{:S(2)}, u32[]{:S(2)}) collective-permute-start(f32[256,128]{1,0:T(8,128)S(1)} %copy-done.7), channel_id=1, source_target_pairs={{0,2},{1,3},{2,0},{3,1},{4,6},{5,7},{6,4},{7,5},{8,10},{9,11},{10,... | collective-permute-start | bytes 393224 | tf_op jit(solution)/shard_map/ppermute | solution.py:307
  80.1 8.9 %collective-permute-start.5 = (f32[256,128]{1,0:T(8,128)S(1)}, f32[256,128]{1,0:T(8,128)S(1)}, u32[]{:S(2)}, u32[]{:S(2)}) collective-permute-start(f32[256,128]{1,0:T(8,128)S(1)} %copy-done.6), channel_id=1, source_target_pairs={{0,3},{1,0},{2,1},{3,2},{4,7},{5,4},{6,5},{7,6},{8,11},{9,8},{10,9... | collective-permute-start | bytes 393224 | tf_op jit(solution)/shard_map/ppermute | solution.py:307
  89.0 17.9 %collective-permute-start.6 = (f32[64,128]{1,0:T(8,128)S(1)}, f32[64,128]{1,0:T(8,128)S(1)}, u32[]{:S(2)}, u32[]{:S(2)}) collective-permute-start(f32[64,128]{1,0:T(8,128)S(1)} %get-tuple-element.26), channel_id=1, source_target_pairs={{0,4},{4,8},{8,12},{12,0},{1,5},{5,9},{9,13},{13,1},{2,6},{6,10},{... | collective-permute-start | bytes 98312 | tf_op jit(solution)/shard_map/ppermute | solution.py:307
  91.1 15.9 %collective-permute-start.7 = (f32[64,128]{1,0:T(8,128)S(1)}, f32[64,128]{1,0:T(8,128)S(1)}, u32[]{:S(2)}, u32[]{:S(2)}) collective-permute-start(f32[64,128]{1,0:T(8,128)S(1)} %get-tuple-element.27), channel_id=1, source_target_pairs={{0,8},{4,12},{8,0},{12,4},{1,9},{5,13},{9,1},{13,5},{2,10},{6,14},... | collective-permute-start | bytes 98312 | tf_op jit(solution)/shard_map/ppermute | solution.py:307
  93.8 13.2 %collective-permute-start.8 = (f32[64,128]{1,0:T(8,128)S(1)}, f32[64,128]{1,0:T(8,128)S(1)}, u32[]{:S(2)}, u32[]{:S(2)}) collective-permute-start(f32[64,128]{1,0:T(8,128)S(1)} %get-tuple-element.28), channel_id=1, source_target_pairs={{0,12},{4,0},{8,4},{12,8},{1,13},{5,1},{9,5},{13,9},{2,14},{6,2},{... | collective-permute-start | bytes 98312 | tf_op jit(solution)/shard_map/ppermute | solution.py:307
